TPU v7x, 512 devices: a whole 4x4x16 slice. The times are simulated.
512 devices in a mesh: grp: 4 (over y), dev: 128 (over z, x, core).
Axes of the slice: x: 4, y: 4, z: 16, core: 2. Of those that a mesh axis runs over, the one named last changes fastest.
Arguments:
- spectrum: float32 [1152, 128, 128], P(None, 'dev'), may hold values from 0.05 to 2
- sea_mask: int32 [128, 128], P('dev'), may hold values 0 or 1
- wind: float32 [2, 128, 128], P(None, 'dev'), may hold values from -24 to 24
- currents: float32 [4, 2, 65536], P('grp', None, 'dev'), may hold values from -6 to 6
- coupling: int32 [4, 65536], P('grp', 'dev'), may hold values from 0 to 16383, as said below
Outputs:
- updated: float32 [1152, 128, 128], P(None, 'dev')
- cell_drift: float32 [4, 2, 65536], P('grp', None, 'dev')
Inputs may be any that keep to these rules, and one draw needn't show every extreme that they name: `coupling`: an ocean cell's entry names the wave point i * 128 + j that it is averaged into and reads its drift from; cell c lies in grid column i with i equal to c // 512 - 1, c // 512 or c // 512 + 1, periodic over 128 columns. `sea_mask`: 1 marks a sea point.
All inputs are finite; a program needn't handle non-finite values. No bound on the sum of `sea_mask` on one device may be relied on, other than what follows from the above.
Results may differ from a plain program's by a relative error of at most 0.00014.
Values sent between devices are 32-bit elements; how exact they have to be, the bound alone decides.
A program may use at most 64 MiB of HBM per device.

v0:
```python
import math

import jax
import jax.numpy as jnp
from jax import lax
from jax.sharding import PartitionSpec as P

NDIR = 32


FIRST_FREQ = 0.04
GROWTH = 1.1
SPEED_TOP = 0.45
CURRENT_TOP = 0.2
WIND_GAIN = 0.03
WHITECAP = 0.3
STEEP_SCALE = 0.4
STOKES_GAIN = 3.0


def from_behind(value, axis, steps):
    count = lax.axis_size(axis)
    pairs = [(source, (source + steps) % count) for source in range(count)]
    return lax.ppermute(value, axis, pairs)


def copy_for_each(x, axis):
    copies = jnp.broadcast_to(x, (lax.axis_size(axis), *x.shape))
    return lax.all_to_all(copies, axis, split_axis=0, concat_axis=0, tiled=True)


def of_everyone(x, axis):
    return copy_for_each(x, axis).sum(axis=0)


def with_halo(cells, sides, width):
    for axis, dim in sides:
        count = lax.axis_size(axis)
        head = lax.slice_in_dim(cells, 0, width, axis=dim)
        tail = lax.slice_in_dim(cells, cells.shape[dim] - width, cells.shape[dim], axis=dim)
        cells = jnp.concatenate(
            [
                lax.ppermute(tail, axis, [(i, (i + 1) % count) for i in range(count)]),
                cells,
                lax.ppermute(head, axis, [((i + 1) % count, i) for i in range(count)]),
            ],
            axis=dim,
        )
    return cells


def bin_tables(bin_index):
    freq_level = (bin_index // NDIR).astype(jnp.float32)
    heading = (bin_index % NDIR).astype(jnp.float32) * (2.0 * math.pi / NDIR)
    frequency = FIRST_FREQ * GROWTH**freq_level
    group_speed = SPEED_TOP * FIRST_FREQ / frequency
    return (frequency, jnp.cos(heading), jnp.sin(heading), group_speed)


def column(values):
    return values[:, None, None]


def sources(energy, sea_frac, wind, mean_current, frequency, cosine_dir, sine_dir):
    energy = energy * sea_frac
    spacing = 0.1 * frequency
    total_energy = jnp.sum(energy * column(spacing), axis=0)
    moment = jnp.sum(energy * column(spacing * frequency), axis=0)
    is_sea = sea_frac > 0.5
    safe_total = jnp.where(is_sea, total_energy, 1.0)
    mean_freq = jnp.where(is_sea, moment / safe_total, 1.0)
    steepness = STEEP_SCALE * total_energy * mean_freq**4
    damping = WHITECAP * (column(frequency) / mean_freq) ** 2 * steepness**2
    along_wind = column(cosine_dir) * (wind[0] - mean_current[0]) + column(sine_dir) * (
        wind[1] - mean_current[1]
    )
    growth = WIND_GAIN * jnp.maximum(0.64 * column(frequency) * along_wind - 1.0, 0.0)
    return energy * (1.0 + growth) / (1.0 + damping)


def transport(
    west_energy,
    centre,
    east_energy,
    west_flow,
    centre_flow,
    east_flow,
    group_speed,
    cosine_dir,
    sine_dir,
    sea_frac,
):
    speed_x = column(group_speed * cosine_dir)
    speed_y = column(group_speed * sine_dir)
    face_east = 0.5 * (speed_x + centre_flow[0] + (speed_x + east_flow[0]))
    face_west = 0.5 * (speed_x + west_flow[0] + (speed_x + centre_flow[0]))
    flux_east = jnp.maximum(face_east, 0.0) * centre + jnp.minimum(face_east, 0.0) * east_energy
    flux_west = jnp.maximum(face_west, 0.0) * west_energy + jnp.minimum(face_west, 0.0) * centre
    speed_north = speed_y + centre_flow[1]
    face_north = 0.5 * (speed_north[:, :, :-1] + speed_north[:, :, 1:])
    flux_north = (
        jnp.maximum(face_north, 0.0) * centre[:, :, :-1]
        + jnp.minimum(face_north, 0.0) * centre[:, :, 1:]
    )
    flux_north = jnp.pad(flux_north, ((0, 0), (0, 0), (1, 1)))
    return sea_frac * (
        centre - (flux_east - flux_west) - (flux_north[:, :, 1:] - flux_north[:, :, :-1])
    )


def stokes_table(frequency, cosine_dir, sine_dir):
    weight = STOKES_GAIN * 0.1 * frequency**4
    return jnp.stack([weight * cosine_dir, weight * sine_dir])


def body(spectrum, sea_mask, wind, currents, coupling):
    bin_count = spectrum.shape[0]
    width_y = spectrum.shape[2]
    devices = lax.axis_size("dev")
    device_index = lax.axis_index("dev")
    is_ocean = lax.axis_index("grp") > 0
    cell_values = jnp.concatenate([currents[0], jnp.ones_like(currents[0, :1])], axis=0)
    cell_values = jnp.where(is_ocean, cell_values, 0.0)
    target_col = coupling[0] // width_y
    target_row = coupling[0] % width_y
    band_slot = (target_col - device_index + devices + 1) % devices
    band_index = band_slot * width_y + target_row
    partial_value = jax.ops.segment_sum(cell_values.T, band_index, num_segments=3 * width_y)
    partial_value = partial_value.T.reshape(3, 3, width_y)
    from_west = from_behind(partial_value[:, 2], "dev", 1)
    from_east = from_behind(partial_value[:, 0], "dev", -1)
    owned_sums = (partial_value[:, 1] + from_west + from_east)[:, None, :]
    group_sums = of_everyone(owned_sums, "grp")
    mean_current = group_sums[:2] / jnp.maximum(group_sums[2], 1.0)
    flow_local = CURRENT_TOP * jnp.tanh(mean_current)
    sea_frac = sea_mask.astype(jnp.float32)
    frequency, cosine_dir, sine_dir, group_speed = bin_tables(
        jnp.arange(bin_count, dtype=jnp.int32)
    )
    forced = sources(spectrum, sea_frac, wind, mean_current, frequency, cosine_dir, sine_dir)
    widened = with_halo(jnp.concatenate([forced, flow_local], axis=0), (("dev", 1),), 1)
    updated = transport(
        widened[:bin_count, 0:1],
        forced,
        widened[:bin_count, 2:3],
        widened[bin_count:, 0:1],
        flow_local,
        widened[bin_count:, 2:3],
        group_speed,
        cosine_dir,
        sine_dir,
        sea_frac,
    )
    stokes_weights = stokes_table(frequency, cosine_dir, sine_dir)
    local_drift = jnp.dot(
        stokes_weights, updated.reshape(bin_count, -1), precision=lax.Precision.HIGHEST
    ).reshape(2, 1, width_y)
    band_drift = with_halo(local_drift, (("dev", 1),), 1)
    cell_drift = band_drift.reshape(2, -1)[:, band_index]
    cell_drift = jnp.where(is_ocean, cell_drift, 0.0)[None]
    return (updated, cell_drift)


def solution(mesh):
    return jax.shard_map(
        body,
        mesh=mesh,
        in_specs=(
            P(None, "dev", None),
            P("dev", None),
            P(None, "dev", None),
            P("grp", None, "dev"),
            P("grp", "dev"),
        ),
        out_specs=(P(None, "dev", None), P("grp", None, "dev")),
        check_vma=False,
    )
```

profile of v0, /device:TPU:8, one launch (start us, length us, event | category | flops | bytes accessed | tf_op | source)
XLA Modules:
  0.0 87.2 jit_solution(5225879815622488592)
XLA Ops:
  0.6 0.0 copy-start.3
  0.6 0.0 copy-start
  0.7 0.8 select_bitcast_fusion.1
  1.4 0.1 copy.21
  1.6 0.7 compare_select_fusion
  2.3 2.3 %scatter_custom_fusion = f32[384,3]{1,0:T(8,128)S(1)} fusion(s32[512]{0:T(512)S(1)} %bitcast.93, f32[512,3]{1,0:T(8,128)S(1)} %copy.21, f32[]{:T(128)} %constant.116.clone.1), kind=kCustom, calls=%fused_computation.32 | custom fusion | flops 1536 | bytes 4612 | tf_op jit(solution)/shard_map/scatter-add | solution.py:128
  4.6 0.0 copy-start.2
  4.6 13.0 %collective-permute-start.1 = (f32[3,128]{0,1:T(8,128)S(1)}, f32[3,128]{0,1:T(8,128)S(1)}, u32[]{:S(2)}, u32[]{:S(2)}) collective-permute-start(f32[3,128]{0,1:T(8,128)S(1)} %get-tuple-element.19), channel_id=1, source_target_pairs={{0,127},{1,0},{2,1},{3,2},{4,3},{5,4},{6,5},{7,6},{8,7},{9,8},{10,... | collective-permute-start | bytes 4616 | tf_op jit(solution)/shard_map/ppermute | solution.py:24
  17.7 1.9 %collective-permute-start = (f32[3,128]{0,1:T(8,128)S(1)}, f32[3,128]{0,1:T(8,128)S(1)}, u32[]{:S(2)}, u32[]{:S(2)}) collective-permute-start(f32[3,128]{0,1:T(8,128)S(1)} %get-tuple-element.18), channel_id=1, source_target_pairs={{0,1},{1,2},{2,3},{3,4},{4,5},{5,6},{6,7},{7,8},{8,9},{9,10},{10,1... | collective-permute-start | bytes 4616 | tf_op jit(solution)/shard_map/ppermute | solution.py:24
  19.6 0.1 fusion.30
  19.7 0.2 sine_multiply_fusion
  19.9 0.0 copy-done.3
  19.9 0.0 copy-done
  19.9 4.3 %multiply_reduce_fusion.1 = (f32[128]{0:T(128)S(1)}, f32[128]{0:T(128)S(1)}) fusion(f32[1152]{0:T(1024)S(1)} %get-tuple-element.25, f32[1152,1,128]{2,1,0:T(1,128)S(1)} %copy-done, f32[128]{0:T(128)S(1)} %convert_bitcast_fusion, f32[1152]{0:T(1024)S(1)} %get-tuple-element.24), kind=kLoop, calls=%fused_computation.27 | loop fusion | flops 737024 | bytes 600576 | tf_op jit(solution)/shard_map/reduce_sum | solution.py:68
  24.2 0.1 fusion.45
  24.3 0.0 collective-permute-done.1
  24.3 2.3 %collective-permute-done = f32[3,128]{0,1:T(8,128)S(1)} collective-permute-done((f32[3,128]{0,1:T(8,128)S(1)}, f32[3,128]{0,1:T(8,128)S(1)}, u32[]{:S(2)}, u32[]{:S(2)}) %collective-permute-start) | collective-permute-done | bytes 1568 | tf_op jit(solution)/shard_map/ppermute | solution.py:24
  26.6 0.1 copy.22
  26.6 0.6 broadcast_in_dim.16
  27.3 4.9 %all-to-all-start = ((f32[4,3,1,128]{3,2,1,0:T(1,128)}), f32[4,3,1,128]{3,2,1,0:T(1,128)S(1)}, u32[]{:S(2)}, u32[]{:S(2)}) async-start(f32[4,3,1,128]{3,2,1,0:T(1,128)} %broadcast_in_dim.16), calls=%async_computation | async-start | bytes 12288 | tf_op jit(solution)/shard_map/all_to_all | solution.py:29
  32.2 0.1 fusion.46
  32.2 3.8 %all-to-all-done = f32[4,3,1,128]{3,2,1,0:T(1,128)S(1)} async-done(((f32[4,3,1,128]{3,2,1,0:T(1,128)}), f32[4,3,1,128]{3,2,1,0:T(1,128)S(1)}, u32[]{:S(2)}, u32[]{:S(2)}) %all-to-all-start) | async-done | bytes 6176 | tf_op jit(solution)/shard_map/all_to_all | solution.py:29
  36.1 0.0 copy-done.2
  36.1 6.3 %fusion.2 = f32[1152,1,128]{2,1,0:T(1,128)S(1)} fusion(f32[1152]{0:T(1024)S(1)} %get-tuple-element.29, f32[128]{0:T(128)S(1)} %get-tuple-element.16, f32[128]{0:T(128)S(1)} %bitcast.90, f32[128]{0:T(128)S(1)} %get-tuple-element.21, f32[128]{0:T(128)S(1)} %get-tuple-element.20, f32[1152]{0:T(1024)S(1)} %get-tuple-element.28, f32[1152]{0:T(1024)S(1)} %get-tuple-element.26, ...), kind=kLoop, calls=%fused_computation.11 | loop fusion | flops 2211840 | bytes 1200640 | tf_op jit(solution)/shard_map/div | solution.py:78
  42.4 1.9 %pad_maximum_fusion = f32[1154,1,128]{2,1,0:T(1,128)S(1)} fusion(f32[2,1,128]{2,1,0:T(1,128)S(1)} %bitcast.88, f32[1152,1,128]{2,1,0:T(1,128)S(1)} %fusion.2), kind=kLoop, calls=%fused_computation.7 | loop fusion | flops 147712 | bytes 1181696 | tf_op jit(solution)/shard_map/concatenate | solution.py:141
  44.3 1.9 %collective-permute-start.3 = (f32[1154,1,128]{2,1,0:T(1,128)S(1)}, f32[1154,1,128]{2,1,0:T(1,128)S(1)}, u32[]{:S(2)}, u32[]{:S(2)}) collective-permute-start(f32[1154,1,128]{2,1,0:T(1,128)S(1)} %pad_maximum_fusion), channel_id=1, source_target_pairs={{0,1},{1,2},{2,3},{3,4},{4,5},{5,6},{6,7},{7,8},{8,9},{9,10},{10,1... | collective-permute-start | bytes 1772552 | tf_op jit(solution)/shard_map/ppermute | solution.py:43
  46.2 7.0 %collective-permute-start.2 = (f32[1154,1,128]{2,1,0:T(1,128)S(1)}, f32[1154,1,128]{2,1,0:T(1,128)S(1)}, u32[]{:S(2)}, u32[]{:S(2)}) collective-permute-start(f32[1154,1,128]{2,1,0:T(1,128)S(1)} %pad_maximum_fusion), channel_id=1, source_target_pairs={{1,0},{2,1},{3,2},{4,3},{5,4},{6,5},{7,6},{8,7},{9,8},{10,9},{11,1... | collective-permute-start | bytes 1772552 | tf_op jit(solution)/shard_map/ppermute | solution.py:45
  53.2 3.3 %broadcast_add_fusion = f32[1152,1,128]{2,1,0:T(1,128)S(1)} fusion(f32[128]{0:T(128)S(1)} %get-tuple-element.23, f32[1152]{0:T(1024)S(1)} %fusion.45), kind=kLoop, calls=%fused_computation.29 | loop fusion | flops 147456 | bytes 594944 | tf_op jit(solution)/shard_map/add | solution.py:99
  56.5 2.6 %fusion.7 = f32[1152,1,127]{2,1,0:T(1,128)S(1)} fusion(f32[1152,1,128]{2,1,0:T(1,128)S(1)} %fusion.2, f32[1152,1,128]{2,1,0:T(1,128)S(1)} %broadcast_add_fusion), kind=kLoop, calls=%fused_computation.17 | loop fusion | flops 1024128 | bytes 2926080 | tf_op jit(solution)/shard_map/add | solution.py:102
  59.1 0.0 collective-permute-done.3
  59.1 1.5 %collective-permute-done.2 = f32[1154,1,128]{2,1,0:T(1,128)S(1)} collective-permute-done((f32[1154,1,128]{2,1,0:T(1,128)S(1)}, f32[1154,1,128]{2,1,0:T(1,128)S(1)}, u32[]{:S(2)}, u32[]{:S(2)}) %collective-permute-start.2) | collective-permute-done | bytes 590880 | tf_op jit(solution)/shard_map/ppermute | solution.py:45
  60.6 8.8 %fusion.12 = f32[1152,1,128]{2,1,0:T(1,128)S(1)} fusion(f32[1152,1,127]{2,1,0:T(1,128)S(1)} %fusion.7, f32[1154,1,128]{2,1,0:T(1,128)S(1)} %collective-permute-done.3, f32[1154,1,128]{2,1,0:T(1,128)S(1)} %collective-permute-done.2, f32[128]{0:T(128)S(1)} %slice_bitcast_fusion.3, f32[128]{0:T(128)S(1)} %slice_bitcast_fusion.4, f32[128]{0:T(128)S(1)} %get-tuple-element.22, ...), kind=kLoop, calls=%fused_computation.28 | loop fusion | flops 5455872 | bytes 2971648 | tf_op jit(solution)/shard_map/mul | solution.py:106
  69.4 0.0 copy-start.1
  69.4 0.4 convolution_bitcast_fusion
  69.9 7.1 %collective-permute-start.5 = (f32[2,1,128]{2,0,1:T(2,128)S(1)}, f32[2,1,128]{2,0,1:T(2,128)S(1)}, u32[]{:S(2)}, u32[]{:S(2)}) collective-permute-start(f32[2,1,128]{2,0,1:T(2,128)S(1)} %convolution_bitcast_fusion), channel_id=1, source_target_pairs={{1,0},{2,1},{3,2},{4,3},{5,4},{6,5},{7,6},{8,7},{9,8},{10,9},{11,1... | collective-permute-start | bytes 3080 | tf_op jit(solution)/shard_map/ppermute | solution.py:45
  77.0 1.9 %collective-permute-start.4 = (f32[2,1,128]{2,0,1:T(2,128)S(1)}, f32[2,1,128]{2,0,1:T(2,128)S(1)}, u32[]{:S(2)}, u32[]{:S(2)}) collective-permute-start(f32[2,1,128]{2,0,1:T(2,128)S(1)} %convolution_bitcast_fusion), channel_id=1, source_target_pairs={{0,1},{1,2},{2,3},{3,4},{4,5},{5,6},{6,7},{7,8},{8,9},{9,10},{10,1... | collective-permute-start | bytes 3080 | tf_op jit(solution)/shard_map/ppermute | solution.py:43
  78.9 0.0 collective-permute-done.5
  79.0 6.3 %collective-permute-done.4 = f32[2,1,128]{2,0,1:T(2,128)S(1)} collective-permute-done((f32[2,1,128]{2,0,1:T(2,128)S(1)}, f32[2,1,128]{2,0,1:T(2,128)S(1)}, u32[]{:S(2)}, u32[]{:S(2)}) %collective-permute-start.4) | collective-permute-done | bytes 1056 | tf_op jit(solution)/shard_map/ppermute | solution.py:43
  85.2 0.1 copy.25
  85.4 1.0 %gather_fusion = f32[512,2]{1,0:T(8,128)S(1)} fusion(f32[2,384]{0,1:T(8,128)S(1)} %copy.25, s32[1024]{0:T(1024)S(1)} %pad_clamp_fusion), kind=kCustom, calls=%fused_computation | custom fusion | bytes 10240 | tf_op jit(solution)/shard_map/gather | solution.py:159
  86.4 0.0 copy-done.1
  86.5 0.7 copy.26
  (16 shorter events, 0.1 us)
Async XLA Ops:
  0.6 19.2 %copy-start.3 = (s32[1,128]{1,0:T(1,128)S(1)}, s32[1,128]{1,0:T(1,128)}, u32[]{:S(2)}) copy-start(s32[1,128]{1,0:T(1,128)} %param.6) | copy-start | bytes 1540
  0.6 19.2 %copy-start = (f32[1152,1,128]{2,1,0:T(1,128)S(1)}, f32[1152,1,128]{2,1,0:T(1,128)}, u32[]{:S(2)}) copy-start(f32[1152,1,128]{2,1,0:T(1,128)} %param.5) | copy-start | bytes 1769476
  4.6 31.5 %copy-start.2 = (f32[2,1,128]{2,1,0:T(1,128)S(1)}, f32[2,1,128]{2,1,0:T(1,128)}, u32[]{:S(2)}) copy-start(f32[2,1,128]{2,1,0:T(1,128)} %param.7) | copy-start | bytes 3076
  4.6 19.7 %collective-permute-start.1 = (f32[3,128]{0,1:T(8,128)S(1)}, f32[3,128]{0,1:T(8,128)S(1)}, u32[]{:S(2)}, u32[]{:S(2)}) collective-permute-start(f32[3,128]{0,1:T(8,128)S(1)} %get-tuple-element.19), channel_id=1, source_target_pairs={{0,127},{1,0},{2,1},{3,2},{4,3},{5,4},{6,5},{7,6},{8,7},{9,8},{10,... | collective-permute-start | bytes 4616 | tf_op jit(solution)/shard_map/ppermute | solution.py:24
  17.7 8.9 %collective-permute-start = (f32[3,128]{0,1:T(8,128)S(1)}, f32[3,128]{0,1:T(8,128)S(1)}, u32[]{:S(2)}, u32[]{:S(2)}) collective-permute-start(f32[3,128]{0,1:T(8,128)S(1)} %get-tuple-element.18), channel_id=1, source_target_pairs={{0,1},{1,2},{2,3},{3,4},{4,5},{5,6},{6,7},{7,8},{8,9},{9,10},{10,1... | collective-permute-start | bytes 4616 | tf_op jit(solution)/shard_map/ppermute | solution.py:24
  27.3 8.8 %all-to-all-start = ((f32[4,3,1,128]{3,2,1,0:T(1,128)}), f32[4,3,1,128]{3,2,1,0:T(1,128)S(1)}, u32[]{:S(2)}, u32[]{:S(2)}) async-start(f32[4,3,1,128]{3,2,1,0:T(1,128)} %broadcast_in_dim.16), calls=%async_computation | async-start | bytes 12288 | tf_op jit(solution)/shard_map/all_to_all | solution.py:29
  44.3 14.8 %collective-permute-start.3 = (f32[1154,1,128]{2,1,0:T(1,128)S(1)}, f32[1154,1,128]{2,1,0:T(1,128)S(1)}, u32[]{:S(2)}, u32[]{:S(2)}) collective-permute-start(f32[1154,1,128]{2,1,0:T(1,128)S(1)} %pad_maximum_fusion), channel_id=1, source_target_pairs={{0,1},{1,2},{2,3},{3,4},{4,5},{5,6},{6,7},{7,8},{8,9},{9,10},{10,1... | collective-permute-start | bytes 1772552 | tf_op jit(solution)/shard_map/ppermute | solution.py:43
  46.2 14.4 %collective-permute-start.2 = (f32[1154,1,128]{2,1,0:T(1,128)S(1)}, f32[1154,1,128]{2,1,0:T(1,128)S(1)}, u32[]{:S(2)}, u32[]{:S(2)}) collective-permute-start(f32[1154,1,128]{2,1,0:T(1,128)S(1)} %pad_maximum_fusion), channel_id=1, source_target_pairs={{1,0},{2,1},{3,2},{4,3},{5,4},{6,5},{7,6},{8,7},{9,8},{10,9},{11,1... | collective-permute-start | bytes 1772552 | tf_op jit(solution)/shard_map/ppermute | solution.py:45
  69.4 17.0 %copy-start.1 = (f32[1152,1,128]{2,1,0:T(1,128)}, f32[1152,1,128]{2,1,0:T(1,128)S(1)}, u32[]{:S(2)}) copy-start(f32[1152,1,128]{2,1,0:T(1,128)S(1)} %fusion.12) | copy-start | bytes 1769476
  69.9 9.1 %collective-permute-start.5 = (f32[2,1,128]{2,0,1:T(2,128)S(1)}, f32[2,1,128]{2,0,1:T(2,128)S(1)}, u32[]{:S(2)}, u32[]{:S(2)}) collective-permute-start(f32[2,1,128]{2,0,1:T(2,128)S(1)} %convolution_bitcast_fusion), channel_id=1, source_target_pairs={{1,0},{2,1},{3,2},{4,3},{5,4},{6,5},{7,6},{8,7},{9,8},{10,9},{11,1... | collective-permute-start | bytes 3080 | tf_op jit(solution)/shard_map/ppermute | solution.py:45
  77.0 8.2 %collective-permute-start.4 = (f32[2,1,128]{2,0,1:T(2,128)S(1)}, f32[2,1,128]{2,0,1:T(2,128)S(1)}, u32[]{:S(2)}, u32[]{:S(2)}) collective-permute-start(f32[2,1,128]{2,0,1:T(2,128)S(1)} %convolution_bitcast_fusion), channel_id=1, source_target_pairs={{0,1},{1,2},{2,3},{3,4},{4,5},{5,6},{6,7},{7,8},{8,9},{9,10},{10,1... | collective-permute-start | bytes 3080 | tf_op jit(solution)/shard_map/ppermute | solution.py:43
where the time goes:
time: 87.5 us; the launch traced here: 87.2 us
  starting transfers between devices  37.8 us (43%)
  other arithmetic  31.4 us (36%)
  waiting for transfers between devices  13.8 us (16%)
  local copies, waits for them, and re-layouts  2.75 us (3%)
  between operations  0.95 us (1%)
    ppermute x2, starting transfers between devices, from_behind(): return lax.ppermute(value, axis, pairs)  15 us
    ppermute x2, starting transfers between devices, with_halo(): lax.ppermute(head, axis, [((i + 1) % count, i) for i in range(count)])  14.1 us
    mul x2, other arithmetic, transport(): sea_frac * (centre - (flux_east - flux_west) - (flux_north[:, :, 1:] - fl...  8.83 us
    div x1, other arithmetic, sources(): return energy * (1.0 + growth) / (1.0 + damping)  6.29 us
    ppermute x2, waiting for transfers between devices, with_halo(): lax.ppermute(tail, axis, [(i, (i + 1) % count) for i in range(count)])  6.26 us
    all_to_all x1, starting transfers between devices, copy_for_each(): return lax.all_to_all(copies, axis, split_axis=0, concat_axis=0, tiled=True)  4.91 us
    reduce_sum x1, other arithmetic, sources(): moment = jnp.sum(energy * column(spacing * frequency), axis=0)  4.33 us
    ppermute x2, starting transfers between devices, with_halo(): lax.ppermute(tail, axis, [(i, (i + 1) % count) for i in range(count)])  3.84 us
  transfers between devices with their start and end apart: 7, of which 4 were waited for; matrix products, arithmetic and copies ran while one was open for 12% of the time, Pallas kernels for 0%

commit v1 on v0

v1 whole, which is shorter than its diff:
```python
import functools
import math

import jax
import jax.numpy as jnp
import numpy as np
from jax import lax
from jax.experimental import pallas as pl
from jax.experimental.pallas import tpu as pltpu
from jax.sharding import PartitionSpec as P

MESH = pl.DeviceIdType.MESH
F32 = jnp.float32
BF16 = jnp.bfloat16

NDIR = 32
FIRST_FREQ = 0.04
GROWTH = 1.1
SPEED_TOP = 0.45
CURRENT_TOP = 0.2
WIND_GAIN = 0.03
WHITECAP = 0.3
STEEP_SCALE = 0.4
STOKES_GAIN = 3.0
LANES = 128
SUB = 8
GROWTH_F = WIND_GAIN * 0.64


def bin_tables(levels):
    padded = -(-levels // SUB) * SUB
    heading = np.arange(NDIR) * (2.0 * math.pi / NDIR)
    freq = FIRST_FREQ * GROWTH ** np.arange(padded)
    rows = np.concatenate(
        [
            np.cos(heading),
            np.sin(heading),
            GROWTH_F * freq,
            freq**2,
            SPEED_TOP * FIRST_FREQ / freq,
            STOKES_GAIN * 0.1 * freq**4,
        ]
    )
    table = np.broadcast_to(rows[:, None], (rows.shape[0], LANES))
    return jnp.asarray(table.astype(np.float32)), padded


def split3(x):
    hi = x.astype(BF16)
    rest = x - hi.astype(F32)
    mid = rest.astype(BF16)
    low = (rest - mid.astype(F32)).astype(BF16)
    return jnp.concatenate([hi, mid, low], axis=0)


def sum3(x):
    n = x.shape[0] // 3
    return x[:n] + x[n : 2 * n] + x[2 * n :]


def kernel(
    n_grp,
    n_dev,
    levels,
    padded,
    chunks,
    head_chunks,
    spec_hbm,
    mask_ref,
    wind_ref,
    cur_ref,
    coup_ref,
    tab_ref,
    upd_ref,
    cell_ref,
    ctr,
    west,
    east,
    base,
    part,
    nbr,
    info,
    drift,
    rtab,
    dtab,
    load_sem,
    halo_send,
    halo_recv,
    part_send,
    part_recv,
    nbr_send,
    nbr_recv,
    info_send,
    info_recv,
    drift_send,
    drift_recv,
):
    g = lax.axis_index("grp")
    d = lax.axis_index("dev")
    bins = levels * NDIR
    per = levels // chunks
    rows = per * NDIR
    quads = NDIR // SUB
    COS, SIN, FG = 0, NDIR, 2 * NDIR
    F2, GS, WT = FG + padded, FG + 2 * padded, FG + 3 * padded

    def at(step):
        return {"grp": g, "dev": lax.rem(d + step + n_dev, n_dev)}

    def group(step):
        return {"grp": lax.rem(g + step, n_grp), "dev": d}

    barrier = pltpu.get_barrier_semaphore()
    for k in range(1, n_grp):
        pl.semaphore_signal(barrier, inc=1, device_id=group(k), device_id_type=MESH)
    for k in (-2, -1, 1, 2):
        pl.semaphore_signal(barrier, inc=1, device_id=at(k), device_id_type=MESH)

    load = pltpu.make_async_copy(spec_hbm, ctr, load_sem)
    load.start()

    coup = coup_ref[...]
    slot = ((coup >> 7) - d + n_dev + 1) & (n_dev - 1)
    row = coup & (LANES - 1)
    cells = coup.shape[1]
    one_hot = jnp.where(
        lax.broadcasted_iota(jnp.int32, (LANES, cells), 0) == row, 1.0, 0.0
    ).astype(BF16)
    kind = lax.broadcasted_iota(jnp.int32, (2 * SUB, cells), 0)
    comp = kind & 3
    value = jnp.where(
        comp == 0, cur_ref[0:1, :], jnp.where(comp == 1, cur_ref[1:2, :], jnp.where(comp == 2, 1.0, 0.0))
    )
    value = jnp.where(jnp.logical_and((kind >> 2) == slot, g > 0), value, 0.0)
    sums = lax.dot_general(
        split3(value), one_hot, (((1,), (1,)), ((), ())), preferred_element_type=F32
    )
    part[g] = sum3(sums)

    load.wait()

    def add_level(l, acc):
        r = pl.multiple_of(l * NDIR, NDIR)
        e = ctr[pl.ds(r, SUB), :]
        for m in range(1, quads):
            e = e + ctr[pl.ds(r + m * SUB, SUB), :]
        return (
            acc[0] + e * tab_ref[pl.ds(FG + l, 1), :],
            acc[1] + e * tab_ref[pl.ds(F2 + l, 1), :],
        )

    zero = jnp.zeros((SUB, LANES), F32)
    total, moment = lax.fori_loop(0, levels, add_level, (zero, zero), unroll=4)
    sea = mask_ref[...].astype(F32)
    total = jnp.sum(total, axis=0, keepdims=True) * (0.1 / GROWTH_F) * sea
    moment = jnp.sum(moment, axis=0, keepdims=True) * 0.1 * sea
    is_sea = sea > 0.5
    mean_freq = jnp.where(is_sea, moment / jnp.where(is_sea, total, 1.0), 1.0)
    steepness = STEEP_SCALE * total * mean_freq**4
    damp = WHITECAP * (steepness / mean_freq) ** 2
    which = lax.broadcasted_iota(jnp.int32, (SUB, LANES), 0)
    info[1] = jnp.where(
        which == 0,
        sea,
        jnp.where(
            which == 1,
            damp,
            jnp.where(which == 2, wind_ref[0:1, :], jnp.where(which == 3, wind_ref[1:2, :], 0.0)),
        ),
    )

    pl.semaphore_wait(barrier, n_grp - 1 + 4)

    part_copies = []
    for k in range(1, n_grp):
        copy = pltpu.make_async_remote_copy(
            src_ref=part.at[g],
            dst_ref=part.at[g],
            send_sem=part_send.at[k],
            recv_sem=part_recv.at[g],
            device_id=group(k),
            device_id_type=MESH,
        )
        copy.start()
        part_copies.append(copy)
    info_copies = []
    for i, step in enumerate((1, -1)):
        copy = pltpu.make_async_remote_copy(
            src_ref=info.at[1],
            dst_ref=info.at[1 - step],
            send_sem=info_send.at[i],
            recv_sem=info_recv.at[i],
            device_id=at(step),
            device_id_type=MESH,
        )
        copy.start()
        info_copies.append(copy)

    halo_copies = []

    def send_chunk(k):
        for i, (step, there) in enumerate(((1, west), (-1, east))):
            copy = pltpu.make_async_remote_copy(
                src_ref=ctr.at[pl.ds(k * rows, rows), :],
                dst_ref=there.at[pl.ds(k * rows, rows), :],
                send_sem=halo_send.at[i, k],
                recv_sem=halo_recv.at[i, k],
                device_id=at(step),
                device_id_type=MESH,
            )
            copy.start()
            halo_copies.append(copy)

    for k in range(head_chunks):
        send_chunk(k)

    for k in range(1, n_grp):
        src = lax.rem(g - k + n_grp, n_grp)
        pltpu.make_async_remote_copy(
            src_ref=part.at[src],
            dst_ref=part.at[src],
            send_sem=part_send.at[k],
            recv_sem=part_recv.at[src],
            device_id=group(k),
            device_id_type=MESH,
        ).wait_recv()
    both = part[1]
    for k in range(2, n_grp):
        both = both + part[k]
    nbr[2] = both
    nbr_copies = []
    for i, step in enumerate((-2, -1, 1, 2)):
        copy = pltpu.make_async_remote_copy(
            src_ref=nbr.at[2],
            dst_ref=nbr.at[2 - step],
            send_sem=nbr_send.at[i],
            recv_sem=nbr_recv.at[i],
            device_id=at(step),
            device_id_type=MESH,
        )
        copy.start()
        nbr_copies.append(copy)
    for k in range(head_chunks, chunks):
        send_chunk(k)

    for copy in info_copies:
        copy.wait_recv()
    for copy in nbr_copies:
        copy.wait_recv()

    cos = [tab_ref[pl.ds(COS + m * SUB, SUB), :] for m in range(quads)]
    sin = [tab_ref[pl.ds(SIN + m * SUB, SUB), :] for m in range(quads)]
    flows = []
    for c in range(3):
        s4 = nbr[c + 1, 4:8, :] + nbr[c, 8:12, :] + nbr[c + 2, 0:4, :]
        count = jnp.maximum(s4[2:3], 1.0)
        mean_x = s4[0:1] / count
        mean_y = s4[1:2] / count
        flows.append((CURRENT_TOP * jnp.tanh(mean_x), CURRENT_TOP * jnp.tanh(mean_y)))
        sea_c = info[c, 0:1, :]
        damp_c = info[c, 1:2, :]
        wx = info[c, 2:3, :] - mean_x
        wy = info[c, 3:4, :] - mean_y
        for m in range(quads):
            dtab[c, pl.ds(m * SUB, SUB), :] = cos[m] * wx + sin[m] * wy
        for q in range(padded // SUB):
            f2 = tab_ref[pl.ds(F2 + q * SUB, SUB), :]
            rtab[c, pl.ds(q * SUB, SUB), :] = sea_c / (1.0 + f2 * damp_c)
    wide = (SUB, LANES)
    face_w = jnp.broadcast_to(0.5 * (flows[0][0] + flows[1][0]), wide)
    face_e = jnp.broadcast_to(0.5 * (flows[1][0] + flows[2][0]), wide)
    flow_y = jnp.broadcast_to(flows[1][1], wide)
    face_n = 0.5 * (flow_y + pltpu.roll(flow_y, LANES - 1, 1))
    sea_w = jnp.broadcast_to(sea, wide)
    inner = lax.broadcasted_iota(jnp.int32, wide, 1) < LANES - 1
    gain = [[dtab[c, pl.ds(m * SUB, SUB), :] for m in range(quads)] for c in range(3)]

    def forced(energy, c, m, fg, rec):
        return energy * (jnp.maximum(gain[c][m] * fg + (1.0 - WIND_GAIN), 1.0) * rec)

    def own_level(l, carry):
        fg = tab_ref[pl.ds(FG + l, 1), :]
        gs = tab_ref[pl.ds(GS + l, 1), :]
        rec = rtab[1, pl.ds(l, 1), :]
        for m in range(quads):
            r = pl.ds(pl.multiple_of(l * NDIR + m * SUB, SUB), SUB)
            e = forced(ctr[r, :], 1, m, fg, rec)
            a = jnp.where(inner, gs * sin[m] + face_n, 0.0)
            flux = a * jnp.where(a > 0.0, e, pltpu.roll(e, LANES - 1, 1))
            own = (e - flux) + pltpu.roll(flux, 1, 1)
            base[0, r, :] = e
            base[1, r, :] = own
        return carry

    lax.fori_loop(0, levels, own_level, 0, unroll=2)

    def edge_level(l, acc):
        fg = tab_ref[pl.ds(FG + l, 1), :]
        gs = tab_ref[pl.ds(GS + l, 1), :]
        wt = tab_ref[pl.ds(WT + l, 1), :]
        rec_w = rtab[0, pl.ds(l, 1), :]
        rec_e = rtab[2, pl.ds(l, 1), :]
        out = []
        for m in range(quads):
            r = pl.ds(pl.multiple_of(l * NDIR + m * SUB, SUB), SUB)
            e = base[0, r, :]
            ew = forced(west[r, :], 0, m, fg, rec_w)
            ee = forced(east[r, :], 2, m, fg, rec_e)
            speed = gs * cos[m]
            a = speed + face_e
            b = speed + face_w
            flux_e = a * jnp.where(a > 0.0, e, ee)
            flux_w = b * jnp.where(b > 0.0, ew, e)
            u = sea_w * (base[1, r, :] - flux_e + flux_w)
            upd_ref[r, :] = u
            out.append(acc[m] + wt * u)
        return tuple(out)

    acc = (zero,) * quads
    for k in range(chunks):
        for copy in halo_copies[2 * k : 2 * k + 2]:
            copy.wait_recv()
        acc = lax.fori_loop(k * per, (k + 1) * per, edge_level, acc, unroll=2)

    dx = acc[0] * cos[0]
    dy = acc[0] * sin[0]
    for m in range(1, quads):
        dx = dx + acc[m] * cos[m]
        dy = dy + acc[m] * sin[m]
    drift[1] = jnp.where(
        which == 0,
        jnp.sum(dx, axis=0, keepdims=True),
        jnp.where(which == 1, jnp.sum(dy, axis=0, keepdims=True), 0.0),
    )
    drift_copies = []
    for i, step in enumerate((1, -1)):
        copy = pltpu.make_async_remote_copy(
            src_ref=drift.at[1],
            dst_ref=drift.at[1 - step],
            send_sem=drift_send.at[i],
            recv_sem=drift_recv.at[i],
            device_id=at(step),
            device_id_type=MESH,
        )
        copy.start()
        drift_copies.append(copy)
    for copy in part_copies + info_copies + nbr_copies + halo_copies:
        copy.wait_send()
    for copy in drift_copies:
        copy.wait()

    band = jnp.zeros((2 * SUB, LANES), F32)
    place = lax.broadcasted_iota(jnp.int32, (2 * SUB, LANES), 0)
    for c in range(3):
        for v in range(2):
            band = jnp.where(place == 4 * c + v, drift[c, v : v + 1, :], band)
    picked = sum3(jnp.dot(split3(band), one_hot, preferred_element_type=F32))
    for v in range(2):
        out = jnp.where(
            slot == 0,
            picked[v : v + 1],
            jnp.where(slot == 1, picked[4 + v : 5 + v], picked[8 + v : 9 + v]),
        )
        cell_ref[v : v + 1, :] = jnp.where(g > 0, out, 0.0)


def body(n_grp, n_dev, spectrum, sea_mask, wind, currents, coupling):
    bins, _, width = spectrum.shape
    levels = bins // NDIR
    cells = currents.shape[2]
    table, padded = bin_tables(levels)
    chunks, head_chunks = 6, 2
    vmem = pl.BlockSpec(memory_space=pltpu.VMEM)
    hbm = pl.BlockSpec(memory_space=pl.ANY)
    dma = pltpu.SemaphoreType.DMA
    updated, cell_drift = pl.pallas_call(
        functools.partial(kernel, n_grp, n_dev, levels, padded, chunks, head_chunks),
        out_shape=(
            jax.ShapeDtypeStruct((bins, width), F32),
            jax.ShapeDtypeStruct((2, cells), F32),
        ),
        in_specs=[hbm, vmem, vmem, vmem, vmem, vmem],
        out_specs=(vmem, vmem),
        scratch_shapes=[
            pltpu.VMEM((bins, width), F32),
            pltpu.VMEM((bins, width), F32),
            pltpu.VMEM((bins, width), F32),
            pltpu.VMEM((2, bins, width), F32),
            pltpu.VMEM((n_grp, 2 * SUB, width), F32),
            pltpu.VMEM((5, 2 * SUB, width), F32),
            pltpu.VMEM((3, SUB, width), F32),
            pltpu.VMEM((3, SUB, width), F32),
            pltpu.VMEM((3, padded, width), F32),
            pltpu.VMEM((3, NDIR, width), F32),
            dma(()),
            dma((2, chunks)),
            dma((2, chunks)),
            dma((n_grp,)),
            dma((n_grp,)),
            dma((4,)),
            dma((4,)),
            dma((2,)),
            dma((2,)),
            dma((2,)),
            dma((2,)),
        ],
        compiler_params=pltpu.CompilerParams(
            collective_id=0, has_side_effects=True, vmem_limit_bytes=32 * 1024 * 1024
        ),
        name="wave_step",
    )(
        spectrum.reshape(bins, width),
        sea_mask,
        wind.reshape(2, width),
        currents.reshape(2, cells),
        coupling,
        table,
    )
    return updated.reshape(bins, 1, width), cell_drift.reshape(1, 2, cells)


def solution(mesh):
    return jax.shard_map(
        functools.partial(body, mesh.shape["grp"], mesh.shape["dev"]),
        mesh=mesh,
        in_specs=(
            P(None, "dev", None),
            P("dev", None),
            P(None, "dev", None),
            P("grp", None, "dev"),
            P("grp", "dev"),
        ),
        out_specs=(P(None, "dev", None), P("grp", None, "dev")),
        check_vma=False,
    )
```

time: 87.5 us -> 34.7 us (0.40)
  starting transfers between devices: 37.8 us -> 0 us
  other arithmetic: 31.4 us -> 0 us
  Pallas kernels: 0 us -> 29.1 us
  waiting for transfers between devices: 13.8 us -> 0 us
  local copies, waits for them, and re-layouts: 2.75 us -> 4.73 us
    ppermute x6 -> x0, starting transfers between devices: 32.9 us -> none  [the longest x2 15 us: from_behind(): return lax.ppermute(value, axis, pairs)]
    pallas_call x0 -> x1, Pallas kernels: none -> 29.1 us  [body(): pl.pallas_call(functools.partial(kernel, n_grp, n_dev, levels, padded, ch...]
    ppermute x6 -> x0, waiting for transfers between devices: 10 us -> none  [the longest x2 6.26 us: with_halo(): lax.ppermute(tail, axis, [(i, (i + 1) % count) for i in range(count)])]
    mul x10 -> x0, other arithmetic: 9.15 us -> none  [the longest x2 8.83 us: transport(): sea_frac * (centre - (flux_east - flux_west) - (flux_north[:, :, 1:] - fl...]
    div x1 -> x0, other arithmetic: 6.29 us -> none  [sources(): return energy * (1.0 + growth) / (1.0 + damping)]
    add x3 -> x0, other arithmetic: 5.88 us -> none  [the longest x1 3.27 us: transport(): speed_north = speed_y + centre_flow[1]]
    all_to_all x1 -> x0, starting transfers between devices: 4.91 us -> none  [copy_for_each(): return lax.all_to_all(copies, axis, split_axis=0, concat_axis=0, tiled=True)]
    reduce_sum x2 -> x0, other arithmetic: 4.35 us -> none  [the longest x1 4.33 us: sources(): moment = jnp.sum(energy * column(spacing * frequency), axis=0)]
  transfers between devices with their start and end apart: 7 -> 0, of which waited for: 4 -> 0; matrix products, arithmetic and copies ran while one was open for 12% -> 0% of each run, Pallas kernels for 0% -> 0%
where the time goes in v1:
time: 34.7 us; the launch traced here: 34.5 us
  Pallas kernels  29.1 us (84%)
  local copies, waits for them, and re-layouts  4.73 us (14%)
  between operations  0.67 us (2%)
    pallas_call x1, Pallas kernels, body(): pl.pallas_call(functools.partial(kernel, n_grp, n_dev, levels, padded, ch...  29.1 us
    unnamed x14, local copies, waits for them, and re-layouts  4.73 us

profile of v1, /device:TPU:8, one launch (start us, length us, event | category | flops | bytes accessed | tf_op | source)
XLA Modules:
  0.0 34.5 jit_solution(10227289179061261114)
XLA Ops:
  0.6 0.0 copy-start.2
  0.6 0.0 copy-start.4
  0.7 0.0 copy-start.5
  0.7 0.7 %copy-done.2 = f32[1,2,512]{2,1,0:T(2,128)S(1)} copy-done((f32[1,2,512]{2,1,0:T(2,128)S(1)}, f32[1,2,512]{2,1,0:T(2,128)}, u32[]{:S(2)}) %copy-start.2) | copy-done | bytes 4120
  1.3 0.0 copy-done.4
  1.3 0.0 copy-done.5
  1.3 0.0 copy-start
  1.3 1.1 %copy-done = f32[1152,1,128]{2,1,0:T(1,128)S(1)} copy-done((f32[1152,1,128]{2,1,0:T(1,128)S(1)}, f32[1152,1,128]{2,1,0:T(1,128)}, u32[]{:S(2)}) %copy-start) | copy-done | bytes 589848
  2.4 0.0 copy-start.1
  2.4 0.9 %copy-done.1 = f32[224,128]{1,0:T(8,128)S(1)} copy-done((f32[224,128]{1,0:T(8,128)S(1)}, f32[224,128]{1,0:T(8,128)}, u32[]{:S(2)}) %copy-start.1) | copy-done | bytes 114712
  3.3 0.0 copy-start.3
  3.3 0.7 %copy-done.3 = s32[1,512]{1,0:T(1,128)S(1)} copy-done((s32[1,512]{1,0:T(1,128)S(1)}, s32[1,512]{1,0:T(1,128)}, u32[]{:S(2)}) %copy-start.3) | copy-done | bytes 2072
  4.0 29.1 %wave_step.1 = (f32[1152,128]{1,0:T(8,128)S(1)}, f32[2,512]{1,0:T(2,128)S(1)}) custom-call(f32[1152,128]{1,0:T(8,128)S(1)} %bitcast.7, s32[1,128]{1,0:T(1,128)S(1)} %copy-done.5, f32[2,128]{1,0:T(2,128)S(1)} %bitcast.11, f32[2,512]{1,0:T(2,128)S(1)} %bitcast.9, s32[1,512]{1,0:T(1,128)S(1)} %copy-done.3, f32[224,128]{1,0:T(8,128)S(1)} %copy-done.1), custom_call_target="tpu_custom_call" | custom-call | tf_op jit(solution)/shard_map/wave_step/pallas_call | solution.py:376
  33.1 0.8 %copy.11 = f32[1152,1,128]{2,1,0:T(1,128)} copy(f32[1152,1,128]{2,1,0:T(1,128)S(1)} %bitcast.8) | data formatting | bytes 1179648
  33.9 0.6 %copy.12 = f32[1,2,512]{2,1,0:T(2,128)} copy(f32[1,2,512]{2,1,0:T(2,128)S(1)} %bitcast.10) | data formatting | bytes 8192
Async XLA Ops:
  0.6 0.7 %copy-start.2 = (f32[1,2,512]{2,1,0:T(2,128)S(1)}, f32[1,2,512]{2,1,0:T(2,128)}, u32[]{:S(2)}) copy-start(f32[1,2,512]{2,1,0:T(2,128)} %param.9) | copy-start | bytes 12292
  0.6 0.7 %copy-start.4 = (f32[2,1,128]{2,1,0:T(1,128)S(1)}, f32[2,1,128]{2,1,0:T(1,128)}, u32[]{:S(2)}) copy-start(f32[2,1,128]{2,1,0:T(1,128)} %param.8) | copy-start | bytes 3076
  0.7 0.7 %copy-start.5 = (s32[1,128]{1,0:T(1,128)S(1)}, s32[1,128]{1,0:T(1,128)}, u32[]{:S(2)}) copy-start(s32[1,128]{1,0:T(1,128)} %mask_ref.1) | copy-start | bytes 1540
  1.3 1.1 %copy-start = (f32[1152,1,128]{2,1,0:T(1,128)S(1)}, f32[1152,1,128]{2,1,0:T(1,128)}, u32[]{:S(2)}) copy-start(f32[1152,1,128]{2,1,0:T(1,128)} %param.6) | copy-start | bytes 1769476
  2.4 0.9 %copy-start.1 = (f32[224,128]{1,0:T(8,128)S(1)}, f32[224,128]{1,0:T(8,128)}, u32[]{:S(2)}) copy-start(f32[224,128]{1,0:T(8,128)} %constant.2.clone.tab_ref) | copy-start | bytes 344068
  3.3 0.7 %copy-start.3 = (s32[1,512]{1,0:T(1,128)S(1)}, s32[1,512]{1,0:T(1,128)}, u32[]{:S(2)}) copy-start(s32[1,512]{1,0:T(1,128)} %coup_ref.1) | copy-start | bytes 6148

commit v2 on v1

--- a/solution.py
+++ b/solution.py
@@ -66,21 +66,25 @@
     chunks,
     head_chunks,
     spec_hbm,
+    mask_hbm,
+    wind_hbm,
+    cur_hbm,
+    coup_hbm,
+    tab_hbm,
+    upd_ref,
+    drift,
+    coup_ref,
+    ctr,
     mask_ref,
     wind_ref,
     cur_ref,
-    coup_ref,
     tab_ref,
-    upd_ref,
-    cell_ref,
-    ctr,
     west,
     east,
     base,
     part,
     nbr,
     info,
-    drift,
     rtab,
     dtab,
     load_sem,
@@ -110,15 +114,29 @@
     def group(step):
         return {"grp": lax.rem(g + step, n_grp), "dev": d}
 
+    loads = [
+        pltpu.make_async_copy(src, dst, load_sem.at[i])
+        for i, (src, dst) in enumerate(
+            (
+                (coup_hbm, coup_ref),
+                (cur_hbm, cur_ref),
+                (spec_hbm, ctr),
+                (tab_hbm, tab_ref),
+                (mask_hbm, mask_ref),
+                (wind_hbm, wind_ref),
+            )
+        )
+    ]
+    for load in loads:
+        load.start()
     barrier = pltpu.get_barrier_semaphore()
     for k in range(1, n_grp):
         pl.semaphore_signal(barrier, inc=1, device_id=group(k), device_id_type=MESH)
     for k in (-2, -1, 1, 2):
         pl.semaphore_signal(barrier, inc=1, device_id=at(k), device_id_type=MESH)
 
-    load = pltpu.make_async_copy(spec_hbm, ctr, load_sem)
-    load.start()
-
+    loads[0].wait()
+    loads[1].wait()
     coup = coup_ref[...]
     slot = ((coup >> 7) - d + n_dev + 1) & (n_dev - 1)
     row = coup & (LANES - 1)
@@ -137,7 +155,8 @@
     )
     part[g] = sum3(sums)
 
-    load.wait()
+    for load in loads[2:]:
+        load.wait()
 
     def add_level(l, acc):
         r = pl.multiple_of(l * NDIR, NDIR)
@@ -349,6 +368,20 @@
     for copy in drift_copies:
         copy.wait()
 
+
+def finish(upd_ref, drift, coup_ref, upd_hbm, cell_hbm, cell_ref, sem):
+    g = lax.axis_index("grp")
+    d = lax.axis_index("dev")
+    n_dev = lax.axis_size("dev")
+    store = pltpu.make_async_copy(upd_ref, upd_hbm, sem.at[0])
+    store.start()
+    coup = coup_ref[...]
+    cells = coup.shape[1]
+    slot = ((coup >> 7) - d + n_dev + 1) & (n_dev - 1)
+    row = coup & (LANES - 1)
+    one_hot = jnp.where(
+        lax.broadcasted_iota(jnp.int32, (LANES, cells), 0) == row, 1.0, 0.0
+    ).astype(BF16)
     band = jnp.zeros((2 * SUB, LANES), F32)
     place = lax.broadcasted_iota(jnp.int32, (2 * SUB, LANES), 0)
     for c in range(3):
@@ -362,6 +395,10 @@
             jnp.where(slot == 1, picked[4 + v : 5 + v], picked[8 + v : 9 + v]),
         )
         cell_ref[v : v + 1, :] = jnp.where(g > 0, out, 0.0)
+    cell_store = pltpu.make_async_copy(cell_ref, cell_hbm, sem.at[1])
+    cell_store.start()
+    cell_store.wait()
+    store.wait()
 
 
 def body(n_grp, n_dev, spectrum, sea_mask, wind, currents, coupling):
@@ -371,28 +408,32 @@
     table, padded = bin_tables(levels)
     chunks, head_chunks = 6, 2
     vmem = pl.BlockSpec(memory_space=pltpu.VMEM)
-    hbm = pl.BlockSpec(memory_space=pl.ANY)
+    hbm = pl.BlockSpec(memory_space=pltpu.HBM)
     dma = pltpu.SemaphoreType.DMA
-    updated, cell_drift = pl.pallas_call(
+    updated, drift, coup = pl.pallas_call(
         functools.partial(kernel, n_grp, n_dev, levels, padded, chunks, head_chunks),
         out_shape=(
             jax.ShapeDtypeStruct((bins, width), F32),
-            jax.ShapeDtypeStruct((2, cells), F32),
+            jax.ShapeDtypeStruct((3, SUB, width), F32),
+            jax.ShapeDtypeStruct((1, cells), jnp.int32),
         ),
-        in_specs=[hbm, vmem, vmem, vmem, vmem, vmem],
-        out_specs=(vmem, vmem),
+        in_specs=[hbm] * 6,
+        out_specs=(vmem, vmem, vmem),
         scratch_shapes=[
             pltpu.VMEM((bins, width), F32),
+            pltpu.VMEM((1, width), jnp.int32),
+            pltpu.VMEM((2, width), F32),
+            pltpu.VMEM((2, cells), F32),
+            pltpu.VMEM(table.shape, F32),
             pltpu.VMEM((bins, width), F32),
             pltpu.VMEM((bins, width), F32),
             pltpu.VMEM((2, bins, width), F32),
             pltpu.VMEM((n_grp, 2 * SUB, width), F32),
             pltpu.VMEM((5, 2 * SUB, width), F32),
             pltpu.VMEM((3, SUB, width), F32),
-            pltpu.VMEM((3, SUB, width), F32),
             pltpu.VMEM((3, padded, width), F32),
             pltpu.VMEM((3, NDIR, width), F32),
-            dma(()),
+            dma((6,)),
             dma((2, chunks)),
             dma((2, chunks)),
             dma((n_grp,)),
@@ -409,13 +450,30 @@
         ),
         name="wave_step",
     )(
-        spectrum.reshape(bins, width),
-        sea_mask,
-        wind.reshape(2, width),
-        currents.reshape(2, cells),
-        coupling,
-        table,
-    )
+        *[
+            pltpu.with_memory_space_constraint(x, pltpu.HBM)
+            for x in (
+                spectrum.reshape(bins, width),
+                sea_mask,
+                wind.reshape(2, width),
+                currents.reshape(2, cells),
+                coupling,
+                table,
+            )
+        ]
+    )
+    updated, cell_drift = pl.pallas_call(
+        finish,
+        out_shape=(
+            jax.ShapeDtypeStruct((bins, width), F32),
+            jax.ShapeDtypeStruct((2, cells), F32),
+        ),
+        in_specs=[vmem, vmem, vmem],
+        out_specs=(hbm, hbm),
+        scratch_shapes=[pltpu.VMEM((2, cells), F32), dma((2,))],
+        compiler_params=pltpu.CompilerParams(vmem_limit_bytes=16 * 1024 * 1024),
+        name="finish",
+    )(updated, drift, coup)
     return updated.reshape(bins, 1, width), cell_drift.reshape(1, 2, cells)
 
 

time: 34.7 us -> 30.6 us (0.88)
  local copies, waits for them, and re-layouts: 4.73 us -> 0 us
  Pallas kernels: 29.1 us -> 29.8 us
    unnamed x14 -> x0, local copies, waits for them, and re-layouts: 4.73 us -> none
    pallas_call x0 -> x1, Pallas kernels: none -> 0.84 us  [body(): pl.pallas_call(finish, out_shape=(jax.ShapeDtypeStruct((bins, width), F32...]
where the time goes in v2:
time: 30.6 us; the launch traced here: 30.4 us
  Pallas kernels  29.8 us (97%)
  between operations  0.64 us (2%)
    pallas_call x1, Pallas kernels, body(): pl.pallas_call(functools.partial(kernel, n_grp, n_dev, levels, padded, ch...  29 us
    pallas_call x1, Pallas kernels, body(): pl.pallas_call(finish, out_shape=(jax.ShapeDtypeStruct((bins, width), F32...  0.84 us

profile of v2, /device:TPU:8, one launch (start us, length us, event | category | flops | bytes accessed | tf_op | source)
XLA Modules:
  0.0 30.4 jit_solution(11602165371238835646)
XLA Ops:
  0.6 29.0 %wave_step.1 = (f32[1152,128]{1,0:T(8,128)S(1)}, f32[3,8,128]{2,1,0:T(8,128)S(1)}, s32[1,512]{1,0:T(1,128)S(1)}) custom-call(f32[1152,128]{1,0:T(8,128)} %bitcast.7, s32[1,128]{1,0:T(1,128)} %mask_hbm.1, f32[2,128]{1,0:T(2,128)} %bitcast.9, f32[2,512]{1,0:T(2,128)} %bitcast.8, s32[1,512]{1,0:T(1,128)} %coup_hbm.1, f32[224,128]{1,0:T(8,128)} %constant.2.clone.tab_hbm), custom_call_target="tpu_custom_call" | custom-call | tf_op jit(solution)/shard_map/wave_step/pallas_call | solution.py:413
  29.6 0.8 %finish.1 = (f32[1152,128]{1,0:T(8,128)}, f32[2,512]{1,0:T(2,128)}) custom-call(f32[1152,128]{1,0:T(8,128)S(1)} %get-tuple-element.7.upd_ref, f32[3,8,128]{2,1,0:T(8,128)S(1)} %get-tuple-element.8.drift, s32[1,512]{1,0:T(1,128)S(1)} %get-tuple-element.9.coup_ref), custom_call_target="tpu_custom_call" | custom-call | tf_op jit(solution)/shard_map/finish/pallas_call | solution.py:465

commit v3 on v2

--- a/solution.py
+++ b/solution.py
@@ -73,8 +73,9 @@
     tab_hbm,
     upd_ref,
     drift,
+    where_ref,
+    ctr,
     coup_ref,
-    ctr,
     mask_ref,
     wind_ref,
     cur_ref,
@@ -154,6 +155,8 @@
         split3(value), one_hot, (((1,), (1,)), ((), ())), preferred_element_type=F32
     )
     part[g] = sum3(sums)
+    where_ref[0:1, :] = jnp.where(g > 0, slot, 3)
+    where_ref[1:2, :] = row
 
     for load in loads[2:]:
         load.wait()
@@ -290,8 +293,11 @@
     face_e = jnp.broadcast_to(0.5 * (flows[1][0] + flows[2][0]), wide)
     flow_y = jnp.broadcast_to(flows[1][1], wide)
     face_n = 0.5 * (flow_y + pltpu.roll(flow_y, LANES - 1, 1))
+    face_s = 0.5 * (flow_y + pltpu.roll(flow_y, 1, 1))
     sea_w = jnp.broadcast_to(sea, wide)
-    inner = lax.broadcasted_iota(jnp.int32, wide, 1) < LANES - 1
+    lane = lax.broadcasted_iota(jnp.int32, wide, 1)
+    has_n = lane < LANES - 1
+    has_s = lane > 0
     gain = [[dtab[c, pl.ds(m * SUB, SUB), :] for m in range(quads)] for c in range(3)]
 
     def forced(energy, c, m, fg, rec):
@@ -304,14 +310,16 @@
         for m in range(quads):
             r = pl.ds(pl.multiple_of(l * NDIR + m * SUB, SUB), SUB)
             e = forced(ctr[r, :], 1, m, fg, rec)
-            a = jnp.where(inner, gs * sin[m] + face_n, 0.0)
-            flux = a * jnp.where(a > 0.0, e, pltpu.roll(e, LANES - 1, 1))
-            own = (e - flux) + pltpu.roll(flux, 1, 1)
+            speed = gs * sin[m]
+            a = jnp.where(has_n, speed + face_n, 0.0)
+            b = jnp.where(has_s, speed + face_s, 0.0)
+            flux_n = a * jnp.where(a > 0.0, e, pltpu.roll(e, LANES - 1, 1))
+            flux_s = b * jnp.where(b > 0.0, pltpu.roll(e, 1, 1), e)
             base[0, r, :] = e
-            base[1, r, :] = own
+            base[1, r, :] = e - flux_n + flux_s
         return carry
 
-    lax.fori_loop(0, levels, own_level, 0, unroll=2)
+    lax.fori_loop(0, levels, own_level, 0, unroll=per)
 
     def edge_level(l, acc):
         fg = tab_ref[pl.ds(FG + l, 1), :]
@@ -339,7 +347,7 @@
     for k in range(chunks):
         for copy in halo_copies[2 * k : 2 * k + 2]:
             copy.wait_recv()
-        acc = lax.fori_loop(k * per, (k + 1) * per, edge_level, acc, unroll=2)
+        acc = lax.fori_loop(k * per, (k + 1) * per, edge_level, acc, unroll=per)
 
     dx = acc[0] * cos[0]
     dy = acc[0] * sin[0]
@@ -369,16 +377,12 @@
         copy.wait()
 
 
-def finish(upd_ref, drift, coup_ref, upd_hbm, cell_hbm, cell_ref, sem):
-    g = lax.axis_index("grp")
-    d = lax.axis_index("dev")
-    n_dev = lax.axis_size("dev")
+def finish(upd_ref, drift, where_ref, upd_hbm, cell_hbm, cell_ref, sem):
     store = pltpu.make_async_copy(upd_ref, upd_hbm, sem.at[0])
     store.start()
-    coup = coup_ref[...]
-    cells = coup.shape[1]
-    slot = ((coup >> 7) - d + n_dev + 1) & (n_dev - 1)
-    row = coup & (LANES - 1)
+    slot = where_ref[0:1, :]
+    row = where_ref[1:2, :]
+    cells = row.shape[1]
     one_hot = jnp.where(
         lax.broadcasted_iota(jnp.int32, (LANES, cells), 0) == row, 1.0, 0.0
     ).astype(BF16)
@@ -389,12 +393,9 @@
             band = jnp.where(place == 4 * c + v, drift[c, v : v + 1, :], band)
     picked = sum3(jnp.dot(split3(band), one_hot, preferred_element_type=F32))
     for v in range(2):
-        out = jnp.where(
-            slot == 0,
-            picked[v : v + 1],
-            jnp.where(slot == 1, picked[4 + v : 5 + v], picked[8 + v : 9 + v]),
-        )
-        cell_ref[v : v + 1, :] = jnp.where(g > 0, out, 0.0)
+        out = jnp.where(slot == 2, picked[8 + v : 9 + v], 0.0)
+        out = jnp.where(slot == 1, picked[4 + v : 5 + v], out)
+        cell_ref[v : v + 1, :] = jnp.where(slot == 0, picked[v : v + 1], out)
     cell_store = pltpu.make_async_copy(cell_ref, cell_hbm, sem.at[1])
     cell_store.start()
     cell_store.wait()
@@ -406,21 +407,22 @@
     levels = bins // NDIR
     cells = currents.shape[2]
     table, padded = bin_tables(levels)
-    chunks, head_chunks = 6, 2
+    chunks, head_chunks = 6, 4
     vmem = pl.BlockSpec(memory_space=pltpu.VMEM)
     hbm = pl.BlockSpec(memory_space=pltpu.HBM)
     dma = pltpu.SemaphoreType.DMA
-    updated, drift, coup = pl.pallas_call(
+    updated, drift, where = pl.pallas_call(
         functools.partial(kernel, n_grp, n_dev, levels, padded, chunks, head_chunks),
         out_shape=(
             jax.ShapeDtypeStruct((bins, width), F32),
             jax.ShapeDtypeStruct((3, SUB, width), F32),
-            jax.ShapeDtypeStruct((1, cells), jnp.int32),
+            jax.ShapeDtypeStruct((2, cells), jnp.int32),
         ),
         in_specs=[hbm] * 6,
         out_specs=(vmem, vmem, vmem),
         scratch_shapes=[
             pltpu.VMEM((bins, width), F32),
+            pltpu.VMEM((1, cells), jnp.int32),
             pltpu.VMEM((1, width), jnp.int32),
             pltpu.VMEM((2, width), F32),
             pltpu.VMEM((2, cells), F32),
@@ -473,7 +475,7 @@
         scratch_shapes=[pltpu.VMEM((2, cells), F32), dma((2,))],
         compiler_params=pltpu.CompilerParams(vmem_limit_bytes=16 * 1024 * 1024),
         name="finish",
-    )(updated, drift, coup)
+    )(updated, drift, where)
     return updated.reshape(bins, 1, width), cell_drift.reshape(1, 2, cells)
 
 

time: 30.6 us -> 28.9 us (0.944)
  Pallas kernels: 29.8 us -> 28.1 us
    pallas_call x1, Pallas kernels: 29 us -> 27.3 us  [body(): pl.pallas_call(functools.partial(kernel, n_grp, n_dev, levels, padded, ch...]
where the time goes in v3:
time: 28.9 us; the launch traced here: 28.7 us
  Pallas kernels  28.1 us (97%)
  between operations  0.64 us (2%)
    pallas_call x1, Pallas kernels, body(): pl.pallas_call(functools.partial(kernel, n_grp, n_dev, levels, padded, ch...  27.3 us
    pallas_call x1, Pallas kernels, body(): pl.pallas_call(finish, out_shape=(jax.ShapeDtypeStruct((bins, width), F32...  0.84 us

profile of v3, /device:TPU:8, one launch (start us, length us, event | category | flops | bytes accessed | tf_op | source)
XLA Modules:
  0.0 28.7 jit_solution(13704060821097344156)
XLA Ops:
  0.6 27.3 %wave_step.1 = (f32[1152,128]{1,0:T(8,128)S(1)}, f32[3,8,128]{2,1,0:T(8,128)S(1)}, s32[2,512]{1,0:T(2,128)S(1)}) custom-call(f32[1152,128]{1,0:T(8,128)} %bitcast.7, s32[1,128]{1,0:T(1,128)} %mask_hbm.1, f32[2,128]{1,0:T(2,128)} %bitcast.9, f32[2,512]{1,0:T(2,128)} %bitcast.8, s32[1,512]{1,0:T(1,128)} %coup_hbm.1, f32[224,128]{1,0:T(8,128)} %constant.2.clone.tab_hbm), custom_call_target="tpu_custom_call" | custom-call | tf_op jit(solution)/shard_map/wave_step/pallas_call | solution.py:414
  27.9 0.8 %finish.1 = (f32[1152,128]{1,0:T(8,128)}, f32[2,512]{1,0:T(2,128)}) custom-call(f32[1152,128]{1,0:T(8,128)S(1)} %get-tuple-element.7.upd_ref, f32[3,8,128]{2,1,0:T(8,128)S(1)} %get-tuple-element.8.drift, s32[2,512]{1,0:T(2,128)S(1)} %get-tuple-element.9.where_ref), custom_call_target="tpu_custom_call" | custom-call | tf_op jit(solution)/shard_map/finish/pallas_call | solution.py:467

commit v4 on v3

--- a/solution.py
+++ b/solution.py
@@ -72,7 +72,7 @@
     coup_hbm,
     tab_hbm,
     upd_ref,
-    drift,
+    drift_ref,
     where_ref,
     ctr,
     coup_ref,
@@ -80,12 +80,14 @@
     wind_ref,
     cur_ref,
     tab_ref,
-    west,
-    east,
+    near,
+    far,
     base,
     part,
     nbr,
     info,
+    drift,
+    last,
     rtab,
     dtab,
     load_sem,
@@ -102,6 +104,8 @@
 ):
     g = lax.axis_index("grp")
     d = lax.axis_index("dev")
+    side = 2 * lax.rem(d, 2) - 1
+
     bins = levels * NDIR
     per = levels // chunks
     rows = per * NDIR
@@ -155,7 +159,7 @@
         split3(value), one_hot, (((1,), (1,)), ((), ())), preferred_element_type=F32
     )
     part[g] = sum3(sums)
-    where_ref[0:1, :] = jnp.where(g > 0, slot, 3)
+    where_ref[0:1, :] = jnp.where(g > 0, 1 + (slot - 1) * side, 3)
     where_ref[1:2, :] = row
 
     for load in loads[2:]:
@@ -206,10 +210,10 @@
         copy.start()
         part_copies.append(copy)
     info_copies = []
-    for i, step in enumerate((1, -1)):
+    for i, step in ((1, side), (0, -side)):
         copy = pltpu.make_async_remote_copy(
             src_ref=info.at[1],
-            dst_ref=info.at[1 - step],
+            dst_ref=info.at[2 * i],
             send_sem=info_send.at[i],
             recv_sem=info_recv.at[i],
             device_id=at(step),
@@ -218,23 +222,32 @@
         copy.start()
         info_copies.append(copy)
 
-    halo_copies = []
-
-    def send_chunk(k):
-        for i, (step, there) in enumerate(((1, west), (-1, east))):
-            copy = pltpu.make_async_remote_copy(
-                src_ref=ctr.at[pl.ds(k * rows, rows), :],
-                dst_ref=there.at[pl.ds(k * rows, rows), :],
-                send_sem=halo_send.at[i, k],
-                recv_sem=halo_recv.at[i, k],
-                device_id=at(step),
-                device_id_type=MESH,
-            )
-            copy.start()
-            halo_copies.append(copy)
-
-    for k in range(head_chunks):
-        send_chunk(k)
+    far_copies = []
+
+    def send_far(k):
+        copy = pltpu.make_async_remote_copy(
+            src_ref=ctr.at[pl.ds(k * rows, rows), :],
+            dst_ref=far.at[pl.ds(k * rows, rows), :],
+            send_sem=halo_send.at[k],
+            recv_sem=halo_recv.at[k],
+            device_id=at(side),
+            device_id_type=MESH,
+        )
+        copy.start()
+        far_copies.append(copy)
+
+    send_far(0)
+    near_copy = pltpu.make_async_remote_copy(
+        src_ref=ctr,
+        dst_ref=near,
+        send_sem=halo_send.at[chunks],
+        recv_sem=halo_recv.at[chunks],
+        device_id=at(-side),
+        device_id_type=MESH,
+    )
+    near_copy.start()
+    for k in range(1, head_chunks):
+        send_far(k)
 
     for k in range(1, n_grp):
         src = lax.rem(g - k + n_grp, n_grp)
@@ -263,7 +276,7 @@
         copy.start()
         nbr_copies.append(copy)
     for k in range(head_chunks, chunks):
-        send_chunk(k)
+        send_far(k)
 
     for copy in info_copies:
         copy.wait_recv()
@@ -273,14 +286,19 @@
     cos = [tab_ref[pl.ds(COS + m * SUB, SUB), :] for m in range(quads)]
     sin = [tab_ref[pl.ds(SIN + m * SUB, SUB), :] for m in range(quads)]
     flows = []
+    seas = []
     for c in range(3):
-        s4 = nbr[c + 1, 4:8, :] + nbr[c, 8:12, :] + nbr[c + 2, 0:4, :]
+        o = (c - 1) * side
+        s4 = nbr[o + 2, 4:8, :] + nbr[o + 1, 8:12, :] + nbr[o + 3, 0:4, :]
         count = jnp.maximum(s4[2:3], 1.0)
         mean_x = s4[0:1] / count
         mean_y = s4[1:2] / count
-        flows.append((CURRENT_TOP * jnp.tanh(mean_x), CURRENT_TOP * jnp.tanh(mean_y)))
+        flows.append(CURRENT_TOP * jnp.tanh(mean_x))
+        if c == 1:
+            flow_y = CURRENT_TOP * jnp.tanh(mean_y)
         sea_c = info[c, 0:1, :]
         damp_c = info[c, 1:2, :]
+        seas.append(sea_c)
         wx = info[c, 2:3, :] - mean_x
         wy = info[c, 3:4, :] - mean_y
         for m in range(quads):
@@ -289,92 +307,107 @@
             f2 = tab_ref[pl.ds(F2 + q * SUB, SUB), :]
             rtab[c, pl.ds(q * SUB, SUB), :] = sea_c / (1.0 + f2 * damp_c)
     wide = (SUB, LANES)
-    face_w = jnp.broadcast_to(0.5 * (flows[0][0] + flows[1][0]), wide)
-    face_e = jnp.broadcast_to(0.5 * (flows[1][0] + flows[2][0]), wide)
-    flow_y = jnp.broadcast_to(flows[1][1], wide)
+    sign = side.astype(F32)
+    face_near = jnp.broadcast_to(-sign * (0.5 * (flows[0] + flows[1])), wide)
+    face_far = jnp.broadcast_to(sign * (0.5 * (flows[1] + flows[2])), wide)
+    flow_y = jnp.broadcast_to(flow_y, wide)
     face_n = 0.5 * (flow_y + pltpu.roll(flow_y, LANES - 1, 1))
     face_s = 0.5 * (flow_y + pltpu.roll(flow_y, 1, 1))
     sea_w = jnp.broadcast_to(sea, wide)
     lane = lax.broadcasted_iota(jnp.int32, wide, 1)
     has_n = lane < LANES - 1
     has_s = lane > 0
+    away = [sign * cos[m] for m in range(quads)]
     gain = [[dtab[c, pl.ds(m * SUB, SUB), :] for m in range(quads)] for c in range(3)]
 
     def forced(energy, c, m, fg, rec):
         return energy * (jnp.maximum(gain[c][m] * fg + (1.0 - WIND_GAIN), 1.0) * rec)
 
-    def own_level(l, carry):
+    def drift_rows(acc):
+        dx = acc[0] * cos[0]
+        dy = acc[0] * sin[0]
+        for m in range(1, quads):
+            dx = dx + acc[m] * cos[m]
+            dy = dy + acc[m] * sin[m]
+        dx = jnp.sum(dx, axis=0, keepdims=True)
+        dy = jnp.sum(dy, axis=0, keepdims=True)
+        return jnp.where(which == 0, dx, jnp.where(which == 1, dy, 0.0))
+
+    def own_level(l, acc):
         fg = tab_ref[pl.ds(FG + l, 1), :]
         gs = tab_ref[pl.ds(GS + l, 1), :]
+        wt = tab_ref[pl.ds(WT + l, 1), :]
         rec = rtab[1, pl.ds(l, 1), :]
+        rec_near = rtab[0, pl.ds(l, 1), :]
+        out = []
         for m in range(quads):
             r = pl.ds(pl.multiple_of(l * NDIR + m * SUB, SUB), SUB)
             e = forced(ctr[r, :], 1, m, fg, rec)
+            other = forced(near[r, :], 0, m, fg, rec_near)
             speed = gs * sin[m]
             a = jnp.where(has_n, speed + face_n, 0.0)
             b = jnp.where(has_s, speed + face_s, 0.0)
+            c = face_near - gs * away[m]
             flux_n = a * jnp.where(a > 0.0, e, pltpu.roll(e, LANES - 1, 1))
             flux_s = b * jnp.where(b > 0.0, pltpu.roll(e, 1, 1), e)
+            u = sea_w * (e - flux_n + flux_s - c * jnp.where(c > 0.0, e, other))
             base[0, r, :] = e
-            base[1, r, :] = e - flux_n + flux_s
-        return carry
-
-    lax.fori_loop(0, levels, own_level, 0, unroll=per)
-
-    def edge_level(l, acc):
+            base[1, r, :] = u
+            out.append(acc[m] + wt * u)
+        return tuple(out)
+
+    near_copy.wait_recv()
+    acc = lax.fori_loop(0, levels, own_level, (zero,) * quads, unroll=6)
+    drift[3] = drift_rows(acc)
+    partial_copy = pltpu.make_async_remote_copy(
+        src_ref=drift.at[3],
+        dst_ref=drift.at[2],
+        send_sem=drift_send.at[1],
+        recv_sem=drift_recv.at[1],
+        device_id=at(side),
+        device_id_type=MESH,
+    )
+    partial_copy.start()
+
+    def far_level(l, acc):
         fg = tab_ref[pl.ds(FG + l, 1), :]
         gs = tab_ref[pl.ds(GS + l, 1), :]
         wt = tab_ref[pl.ds(WT + l, 1), :]
-        rec_w = rtab[0, pl.ds(l, 1), :]
-        rec_e = rtab[2, pl.ds(l, 1), :]
+        rec = rtab[2, pl.ds(l, 1), :]
         out = []
         for m in range(quads):
             r = pl.ds(pl.multiple_of(l * NDIR + m * SUB, SUB), SUB)
-            e = base[0, r, :]
-            ew = forced(west[r, :], 0, m, fg, rec_w)
-            ee = forced(east[r, :], 2, m, fg, rec_e)
-            speed = gs * cos[m]
-            a = speed + face_e
-            b = speed + face_w
-            flux_e = a * jnp.where(a > 0.0, e, ee)
-            flux_w = b * jnp.where(b > 0.0, ew, e)
-            u = sea_w * (base[1, r, :] - flux_e + flux_w)
-            upd_ref[r, :] = u
-            out.append(acc[m] + wt * u)
+            other = forced(far[r, :], 2, m, fg, rec)
+            a = gs * away[m] + face_far
+            flux = a * jnp.where(a > 0.0, base[0, r, :], other)
+            upd_ref[r, :] = base[1, r, :] - sea_w * flux
+            out.append(acc[m] + wt * flux)
         return tuple(out)
 
     acc = (zero,) * quads
     for k in range(chunks):
-        for copy in halo_copies[2 * k : 2 * k + 2]:
-            copy.wait_recv()
-        acc = lax.fori_loop(k * per, (k + 1) * per, edge_level, acc, unroll=per)
-
-    dx = acc[0] * cos[0]
-    dy = acc[0] * sin[0]
-    for m in range(1, quads):
-        dx = dx + acc[m] * cos[m]
-        dy = dy + acc[m] * sin[m]
-    drift[1] = jnp.where(
-        which == 0,
-        jnp.sum(dx, axis=0, keepdims=True),
-        jnp.where(which == 1, jnp.sum(dy, axis=0, keepdims=True), 0.0),
-    )
-    drift_copies = []
-    for i, step in enumerate((1, -1)):
-        copy = pltpu.make_async_remote_copy(
-            src_ref=drift.at[1],
-            dst_ref=drift.at[1 - step],
-            send_sem=drift_send.at[i],
-            recv_sem=drift_recv.at[i],
-            device_id=at(step),
-            device_id_type=MESH,
-        )
-        copy.start()
-        drift_copies.append(copy)
-    for copy in part_copies + info_copies + nbr_copies + halo_copies:
+        far_copies[k].wait_recv()
+        acc = lax.fori_loop(k * per, (k + 1) * per, far_level, acc, unroll=per)
+
+    shared = drift_rows(acc)
+    drift[1] = drift[3] - sea * shared
+    full_copy = pltpu.make_async_remote_copy(
+        src_ref=drift.at[1],
+        dst_ref=drift.at[0],
+        send_sem=drift_send.at[0],
+        recv_sem=drift_recv.at[0],
+        device_id=at(-side),
+        device_id_type=MESH,
+    )
+    full_copy.start()
+    partial_copy.wait_recv()
+    last[...] = drift[2] + seas[2] * shared
+    for copy in part_copies + info_copies + nbr_copies + far_copies + [near_copy, partial_copy]:
         copy.wait_send()
-    for copy in drift_copies:
-        copy.wait()
+    full_copy.wait()
+    drift_ref[0] = drift[0]
+    drift_ref[1] = drift[1]
+    drift_ref[2] = last[...]
 
 
 def finish(upd_ref, drift, where_ref, upd_hbm, cell_hbm, cell_ref, sem):
@@ -407,7 +440,7 @@
     levels = bins // NDIR
     cells = currents.shape[2]
     table, padded = bin_tables(levels)
-    chunks, head_chunks = 6, 4
+    chunks, head_chunks = 9, 5
     vmem = pl.BlockSpec(memory_space=pltpu.VMEM)
     hbm = pl.BlockSpec(memory_space=pltpu.HBM)
     dma = pltpu.SemaphoreType.DMA
@@ -433,11 +466,13 @@
             pltpu.VMEM((n_grp, 2 * SUB, width), F32),
             pltpu.VMEM((5, 2 * SUB, width), F32),
             pltpu.VMEM((3, SUB, width), F32),
+            pltpu.VMEM((4, SUB, width), F32),
+            pltpu.VMEM((SUB, width), F32),
             pltpu.VMEM((3, padded, width), F32),
             pltpu.VMEM((3, NDIR, width), F32),
             dma((6,)),
-            dma((2, chunks)),
-            dma((2, chunks)),
+            dma((chunks + 1,)),
+            dma((chunks + 1,)),
             dma((n_grp,)),
             dma((n_grp,)),
             dma((4,)),

time: 28.9 us -> 27.4 us (0.948)
  Pallas kernels: 28.1 us -> 26.7 us
    pallas_call x1, Pallas kernels: 27.3 us -> 25.8 us  [body(): pl.pallas_call(functools.partial(kernel, n_grp, n_dev, levels, padded, ch...]
where the time goes in v4:
time: 27.4 us; the launch traced here: 27.3 us
  Pallas kernels  26.7 us (97%)
  between operations  0.64 us (2%)
    pallas_call x1, Pallas kernels, body(): pl.pallas_call(functools.partial(kernel, n_grp, n_dev, levels, padded, ch...  25.8 us
    pallas_call x1, Pallas kernels, body(): pl.pallas_call(finish, out_shape=(jax.ShapeDtypeStruct((bins, width), F32...  0.84 us

profile of v4, /device:TPU:8, one launch (start us, length us, event | category | flops | bytes accessed | tf_op | source)
XLA Modules:
  0.0 27.3 jit_solution(10777969395608417802)
XLA Ops:
  0.6 25.8 %wave_step.1 = (f32[1152,128]{1,0:T(8,128)S(1)}, f32[3,8,128]{2,1,0:T(8,128)S(1)}, s32[2,512]{1,0:T(2,128)S(1)}) custom-call(f32[1152,128]{1,0:T(8,128)} %bitcast.7, s32[1,128]{1,0:T(1,128)} %mask_hbm.1, f32[2,128]{1,0:T(2,128)} %bitcast.9, f32[2,512]{1,0:T(2,128)} %bitcast.8, s32[1,512]{1,0:T(1,128)} %coup_hbm.1, f32[224,128]{1,0:T(8,128)} %constant.2.clone.tab_hbm), custom_call_target="tpu_custom_call" | custom-call | tf_op jit(solution)/shard_map/wave_step/pallas_call | solution.py:447
  26.5 0.8 %finish.1 = (f32[1152,128]{1,0:T(8,128)}, f32[2,512]{1,0:T(2,128)}) custom-call(f32[1152,128]{1,0:T(8,128)S(1)} %get-tuple-element.7.upd_ref, f32[3,8,128]{2,1,0:T(8,128)S(1)} %get-tuple-element.8.drift, s32[2,512]{1,0:T(2,128)S(1)} %get-tuple-element.9.where_ref), custom_call_target="tpu_custom_call" | custom-call | tf_op jit(solution)/shard_map/finish/pallas_call | solution.py:502

commit v5 on v4

--- a/solution.py
+++ b/solution.py
@@ -64,7 +64,6 @@
     levels,
     padded,
     chunks,
-    head_chunks,
     spec_hbm,
     mask_hbm,
     wind_hbm,
@@ -84,21 +83,20 @@
     far,
     base,
     part,
-    nbr,
-    info,
+    link,
+    sums,
     drift,
     last,
     rtab,
-    dtab,
     load_sem,
     halo_send,
     halo_recv,
     part_send,
     part_recv,
-    nbr_send,
-    nbr_recv,
-    info_send,
-    info_recv,
+    link_send,
+    link_recv,
+    sums_send,
+    sums_recv,
     drift_send,
     drift_recv,
 ):
@@ -137,8 +135,8 @@
     barrier = pltpu.get_barrier_semaphore()
     for k in range(1, n_grp):
         pl.semaphore_signal(barrier, inc=1, device_id=group(k), device_id_type=MESH)
-    for k in (-2, -1, 1, 2):
-        pl.semaphore_signal(barrier, inc=1, device_id=at(k), device_id_type=MESH)
+    for step in (-side, side):
+        pl.semaphore_signal(barrier, inc=1, device_id=at(step), device_id_type=MESH)
 
     loads[0].wait()
     loads[1].wait()
@@ -155,10 +153,13 @@
         comp == 0, cur_ref[0:1, :], jnp.where(comp == 1, cur_ref[1:2, :], jnp.where(comp == 2, 1.0, 0.0))
     )
     value = jnp.where(jnp.logical_and((kind >> 2) == slot, g > 0), value, 0.0)
-    sums = lax.dot_general(
-        split3(value), one_hot, (((1,), (1,)), ((), ())), preferred_element_type=F32
-    )
-    part[g] = sum3(sums)
+    cell_sums = sum3(
+        lax.dot_general(
+            split3(value), one_hot, (((1,), (1,)), ((), ())), preferred_element_type=F32
+        )
+    )
+    link[1, 0 : 2 * SUB, :] = cell_sums
+    part[g] = jnp.zeros((SUB, LANES), F32)
     where_ref[0:1, :] = jnp.where(g > 0, 1 + (slot - 1) * side, 3)
     where_ref[1:2, :] = row
 
@@ -185,7 +186,7 @@
     steepness = STEEP_SCALE * total * mean_freq**4
     damp = WHITECAP * (steepness / mean_freq) ** 2
     which = lax.broadcasted_iota(jnp.int32, (SUB, LANES), 0)
-    info[1] = jnp.where(
+    link[1, 2 * SUB :, :] = jnp.where(
         which == 0,
         sea,
         jnp.where(
@@ -195,8 +196,59 @@
         ),
     )
 
-    pl.semaphore_wait(barrier, n_grp - 1 + 4)
-
+    pl.semaphore_wait(barrier, n_grp - 1 + 2)
+
+    def to_sides(buf, send_sem, recv_sem):
+        copies = []
+        for i, step in ((1, side), (0, -side)):
+            copy = pltpu.make_async_remote_copy(
+                src_ref=buf.at[1],
+                dst_ref=buf.at[2 * i],
+                send_sem=send_sem.at[i],
+                recv_sem=recv_sem.at[i],
+                device_id=at(step),
+                device_id_type=MESH,
+            )
+            copy.start()
+            copies.append(copy)
+        return copies
+
+    link_copies = to_sides(link, link_send, link_recv)
+
+    far_copies = []
+
+    def send_far(k):
+        copy = pltpu.make_async_remote_copy(
+            src_ref=ctr.at[pl.ds(k * rows, rows), :],
+            dst_ref=far.at[pl.ds(k * rows, rows), :],
+            send_sem=halo_send.at[k],
+            recv_sem=halo_recv.at[k],
+            device_id=at(side),
+            device_id_type=MESH,
+        )
+        copy.start()
+        far_copies.append(copy)
+
+    send_far(0)
+    near_copy = pltpu.make_async_remote_copy(
+        src_ref=ctr,
+        dst_ref=near,
+        send_sem=halo_send.at[chunks],
+        recv_sem=halo_recv.at[chunks],
+        device_id=at(-side),
+        device_id_type=MESH,
+    )
+    near_copy.start()
+    for k in range(1, chunks):
+        send_far(k)
+
+    for copy in link_copies:
+        copy.wait_recv()
+    part[g, 0:4, :] = (
+        cell_sums[4:8]
+        + jnp.where(side > 0, link[0, 8:12, :], link[0, 0:4, :])
+        + jnp.where(side > 0, link[2, 0:4, :], link[2, 8:12, :])
+    )
     part_copies = []
     for k in range(1, n_grp):
         copy = pltpu.make_async_remote_copy(
@@ -209,46 +261,6 @@
         )
         copy.start()
         part_copies.append(copy)
-    info_copies = []
-    for i, step in ((1, side), (0, -side)):
-        copy = pltpu.make_async_remote_copy(
-            src_ref=info.at[1],
-            dst_ref=info.at[2 * i],
-            send_sem=info_send.at[i],
-            recv_sem=info_recv.at[i],
-            device_id=at(step),
-            device_id_type=MESH,
-        )
-        copy.start()
-        info_copies.append(copy)
-
-    far_copies = []
-
-    def send_far(k):
-        copy = pltpu.make_async_remote_copy(
-            src_ref=ctr.at[pl.ds(k * rows, rows), :],
-            dst_ref=far.at[pl.ds(k * rows, rows), :],
-            send_sem=halo_send.at[k],
-            recv_sem=halo_recv.at[k],
-            device_id=at(side),
-            device_id_type=MESH,
-        )
-        copy.start()
-        far_copies.append(copy)
-
-    send_far(0)
-    near_copy = pltpu.make_async_remote_copy(
-        src_ref=ctr,
-        dst_ref=near,
-        send_sem=halo_send.at[chunks],
-        recv_sem=halo_recv.at[chunks],
-        device_id=at(-side),
-        device_id_type=MESH,
-    )
-    near_copy.start()
-    for k in range(1, head_chunks):
-        send_far(k)
-
     for k in range(1, n_grp):
         src = lax.rem(g - k + n_grp, n_grp)
         pltpu.make_async_remote_copy(
@@ -262,54 +274,34 @@
     both = part[1]
     for k in range(2, n_grp):
         both = both + part[k]
-    nbr[2] = both
-    nbr_copies = []
-    for i, step in enumerate((-2, -1, 1, 2)):
-        copy = pltpu.make_async_remote_copy(
-            src_ref=nbr.at[2],
-            dst_ref=nbr.at[2 - step],
-            send_sem=nbr_send.at[i],
-            recv_sem=nbr_recv.at[i],
-            device_id=at(step),
-            device_id_type=MESH,
-        )
-        copy.start()
-        nbr_copies.append(copy)
-    for k in range(head_chunks, chunks):
-        send_far(k)
-
-    for copy in info_copies:
-        copy.wait_recv()
-    for copy in nbr_copies:
-        copy.wait_recv()
+    sums[1] = both
+    sums_copies = to_sides(sums, sums_send, sums_recv)
 
     cos = [tab_ref[pl.ds(COS + m * SUB, SUB), :] for m in range(quads)]
     sin = [tab_ref[pl.ds(SIN + m * SUB, SUB), :] for m in range(quads)]
-    flows = []
-    seas = []
-    for c in range(3):
-        o = (c - 1) * side
-        s4 = nbr[o + 2, 4:8, :] + nbr[o + 1, 8:12, :] + nbr[o + 3, 0:4, :]
+    gain = {}
+
+    def column(c, s4):
         count = jnp.maximum(s4[2:3], 1.0)
         mean_x = s4[0:1] / count
         mean_y = s4[1:2] / count
-        flows.append(CURRENT_TOP * jnp.tanh(mean_x))
-        if c == 1:
-            flow_y = CURRENT_TOP * jnp.tanh(mean_y)
-        sea_c = info[c, 0:1, :]
-        damp_c = info[c, 1:2, :]
-        seas.append(sea_c)
-        wx = info[c, 2:3, :] - mean_x
-        wy = info[c, 3:4, :] - mean_y
-        for m in range(quads):
-            dtab[c, pl.ds(m * SUB, SUB), :] = cos[m] * wx + sin[m] * wy
+        row = 2 * SUB
+        sea_c = link[c, row : row + 1, :]
+        damp_c = link[c, row + 1 : row + 2, :]
+        wx = link[c, row + 2 : row + 3, :] - mean_x
+        wy = link[c, row + 3 : row + 4, :] - mean_y
+        gain[c] = [cos[m] * wx + sin[m] * wy for m in range(quads)]
         for q in range(padded // SUB):
             f2 = tab_ref[pl.ds(F2 + q * SUB, SUB), :]
             rtab[c, pl.ds(q * SUB, SUB), :] = sea_c / (1.0 + f2 * damp_c)
+        return CURRENT_TOP * jnp.tanh(mean_x), CURRENT_TOP * jnp.tanh(mean_y), sea_c
+
+    flow_x, flow_y, _ = column(1, both)
+    sums_copies[1].wait_recv()
+    flow_near, _, _ = column(0, sums[0])
     wide = (SUB, LANES)
     sign = side.astype(F32)
-    face_near = jnp.broadcast_to(-sign * (0.5 * (flows[0] + flows[1])), wide)
-    face_far = jnp.broadcast_to(sign * (0.5 * (flows[1] + flows[2])), wide)
+    face_near = jnp.broadcast_to(-sign * (0.5 * (flow_near + flow_x)), wide)
     flow_y = jnp.broadcast_to(flow_y, wide)
     face_n = 0.5 * (flow_y + pltpu.roll(flow_y, LANES - 1, 1))
     face_s = 0.5 * (flow_y + pltpu.roll(flow_y, 1, 1))
@@ -318,7 +310,6 @@
     has_n = lane < LANES - 1
     has_s = lane > 0
     away = [sign * cos[m] for m in range(quads)]
-    gain = [[dtab[c, pl.ds(m * SUB, SUB), :] for m in range(quads)] for c in range(3)]
 
     def forced(energy, c, m, fg, rec):
         return energy * (jnp.maximum(gain[c][m] * fg + (1.0 - WIND_GAIN), 1.0) * rec)
@@ -369,6 +360,10 @@
     )
     partial_copy.start()
 
+    sums_copies[0].wait_recv()
+    flow_far, _, sea_far = column(2, sums[2])
+    face_far = jnp.broadcast_to(sign * (0.5 * (flow_x + flow_far)), wide)
+
     def far_level(l, acc):
         fg = tab_ref[pl.ds(FG + l, 1), :]
         gs = tab_ref[pl.ds(GS + l, 1), :]
@@ -401,8 +396,8 @@
     )
     full_copy.start()
     partial_copy.wait_recv()
-    last[...] = drift[2] + seas[2] * shared
-    for copy in part_copies + info_copies + nbr_copies + far_copies + [near_copy, partial_copy]:
+    last[...] = drift[2] + sea_far * shared
+    for copy in part_copies + link_copies + sums_copies + far_copies + [near_copy, partial_copy]:
         copy.wait_send()
     full_copy.wait()
     drift_ref[0] = drift[0]
@@ -440,12 +435,12 @@
     levels = bins // NDIR
     cells = currents.shape[2]
     table, padded = bin_tables(levels)
-    chunks, head_chunks = 9, 5
+    chunks = 6
     vmem = pl.BlockSpec(memory_space=pltpu.VMEM)
     hbm = pl.BlockSpec(memory_space=pltpu.HBM)
     dma = pltpu.SemaphoreType.DMA
     updated, drift, where = pl.pallas_call(
-        functools.partial(kernel, n_grp, n_dev, levels, padded, chunks, head_chunks),
+        functools.partial(kernel, n_grp, n_dev, levels, padded, chunks),
         out_shape=(
             jax.ShapeDtypeStruct((bins, width), F32),
             jax.ShapeDtypeStruct((3, SUB, width), F32),
@@ -463,20 +458,19 @@
             pltpu.VMEM((bins, width), F32),
             pltpu.VMEM((bins, width), F32),
             pltpu.VMEM((2, bins, width), F32),
-            pltpu.VMEM((n_grp, 2 * SUB, width), F32),
-            pltpu.VMEM((5, 2 * SUB, width), F32),
+            pltpu.VMEM((n_grp, SUB, width), F32),
+            pltpu.VMEM((3, 3 * SUB, width), F32),
             pltpu.VMEM((3, SUB, width), F32),
             pltpu.VMEM((4, SUB, width), F32),
             pltpu.VMEM((SUB, width), F32),
             pltpu.VMEM((3, padded, width), F32),
-            pltpu.VMEM((3, NDIR, width), F32),
             dma((6,)),
             dma((chunks + 1,)),
             dma((chunks + 1,)),
             dma((n_grp,)),
             dma((n_grp,)),
-            dma((4,)),
-            dma((4,)),
+            dma((2,)),
+            dma((2,)),
             dma((2,)),
             dma((2,)),
             dma((2,)),

time: 27.4 us -> 28 us (1.022)
  the two profiles are of different devices: /device:TPU:8 before, /device:TPU:1 now
where the time goes in v5:
time: 28 us; the launch traced here: 27.9 us
  Pallas kernels  27.2 us (97%)
  between operations  0.64 us (2%)
    pallas_call x1, Pallas kernels, body(): pl.pallas_call(functools.partial(kernel, n_grp, n_dev, levels, padded, ch...  26.4 us
    pallas_call x1, Pallas kernels, body(): pl.pallas_call(finish, out_shape=(jax.ShapeDtypeStruct((bins, width), F32...  0.84 us

profile of v5, /device:TPU:1, one launch (start us, length us, event | category | flops | bytes accessed | tf_op | source)
XLA Modules:
  0.0 27.9 jit_solution(5523073732359756741)
XLA Ops:
  0.6 26.4 %wave_step.1 = (f32[1152,128]{1,0:T(8,128)S(1)}, f32[3,8,128]{2,1,0:T(8,128)S(1)}, s32[2,512]{1,0:T(2,128)S(1)}) custom-call(f32[1152,128]{1,0:T(8,128)} %bitcast.7, s32[1,128]{1,0:T(1,128)} %mask_hbm.1, f32[2,128]{1,0:T(2,128)} %bitcast.9, f32[2,512]{1,0:T(2,128)} %bitcast.8, s32[1,512]{1,0:T(1,128)} %coup_hbm.1, f32[224,128]{1,0:T(8,128)} %constant.2.clone.tab_hbm), custom_call_target="tpu_custom_call" | custom-call | tf_op jit(solution)/shard_map/wave_step/pallas_call | solution.py:442
  27.0 0.8 %finish.1 = (f32[1152,128]{1,0:T(8,128)}, f32[2,512]{1,0:T(2,128)}) custom-call(f32[1152,128]{1,0:T(8,128)S(1)} %get-tuple-element.7.upd_ref, f32[3,8,128]{2,1,0:T(8,128)S(1)} %get-tuple-element.8.drift, s32[2,512]{1,0:T(2,128)S(1)} %get-tuple-element.9.where_ref), custom_call_target="tpu_custom_call" | custom-call | tf_op jit(solution)/shard_map/finish/pallas_call | solution.py:496

commit v6 on v5

--- a/solution.py
+++ b/solution.py
@@ -64,6 +64,7 @@
     levels,
     padded,
     chunks,
+    head_chunks,
     spec_hbm,
     mask_hbm,
     wind_hbm,
@@ -159,7 +160,8 @@
         )
     )
     link[1, 0 : 2 * SUB, :] = cell_sums
-    part[g] = jnp.zeros((SUB, LANES), F32)
+    part[1, g] = jnp.zeros((SUB, LANES), F32)
+    sums[1] = jnp.zeros((SUB, LANES), F32)
     where_ref[0:1, :] = jnp.where(g > 0, 1 + (slot - 1) * side, 3)
     where_ref[1:2, :] = row
 
@@ -229,6 +231,40 @@
         copy.start()
         far_copies.append(copy)
 
+    def pick(buf, east, west):
+        return jnp.where(side > 0, buf[east : east + 4], buf[west : west + 4])
+
+    def to_groups(n):
+        copies = []
+        for k in range(1, n_grp):
+            copy = pltpu.make_async_remote_copy(
+                src_ref=part.at[n, g],
+                dst_ref=part.at[n, g],
+                send_sem=part_send.at[n, k],
+                recv_sem=part_recv.at[n, g],
+                device_id=group(k),
+                device_id_type=MESH,
+            )
+            copy.start()
+            copies.append(copy)
+        return copies
+
+    def over_groups(n):
+        for k in range(1, n_grp):
+            src = lax.rem(g - k + n_grp, n_grp)
+            pltpu.make_async_remote_copy(
+                src_ref=part.at[n, src],
+                dst_ref=part.at[n, src],
+                send_sem=part_send.at[n, k],
+                recv_sem=part_recv.at[n, src],
+                device_id=group(k),
+                device_id_type=MESH,
+            ).wait_recv()
+        both = part[n, 1]
+        for k in range(2, n_grp):
+            both = both + part[n, k]
+        return both
+
     send_far(0)
     near_copy = pltpu.make_async_remote_copy(
         src_ref=ctr,
@@ -239,43 +275,40 @@
         device_id_type=MESH,
     )
     near_copy.start()
-    for k in range(1, chunks):
+    for k in range(1, head_chunks):
         send_far(k)
 
-    for copy in link_copies:
-        copy.wait_recv()
-    part[g, 0:4, :] = (
-        cell_sums[4:8]
-        + jnp.where(side > 0, link[0, 8:12, :], link[0, 0:4, :])
-        + jnp.where(side > 0, link[2, 0:4, :], link[2, 8:12, :])
-    )
-    part_copies = []
-    for k in range(1, n_grp):
-        copy = pltpu.make_async_remote_copy(
-            src_ref=part.at[g],
-            dst_ref=part.at[g],
-            send_sem=part_send.at[k],
-            recv_sem=part_recv.at[g],
-            device_id=group(k),
-            device_id_type=MESH,
-        )
-        copy.start()
-        part_copies.append(copy)
-    for k in range(1, n_grp):
-        src = lax.rem(g - k + n_grp, n_grp)
-        pltpu.make_async_remote_copy(
-            src_ref=part.at[src],
-            dst_ref=part.at[src],
-            send_sem=part_send.at[k],
-            recv_sem=part_recv.at[src],
-            device_id=group(k),
-            device_id_type=MESH,
-        ).wait_recv()
-    both = part[1]
-    for k in range(2, n_grp):
-        both = both + part[k]
-    sums[1] = both
-    sums_copies = to_sides(sums, sums_send, sums_recv)
+    link_copies[1].wait_recv()
+    part[0, g, 0:4, :] = cell_sums[4:8] + pick(link[0], 8, 0)
+    part[0, g, 4:8, :] = pick(cell_sums, 8, 0)
+    part_copies = to_groups(0)
+    link_copies[0].wait_recv()
+    part[1, g, 0:4, :] = pick(link[2], 0, 8)
+    part_copies += to_groups(1)
+    chip = over_groups(0)
+    sums[3] = chip
+    chip_copy = pltpu.make_async_remote_copy(
+        src_ref=sums.at[3],
+        dst_ref=sums.at[2],
+        send_sem=sums_send.at[1],
+        recv_sem=sums_recv.at[1],
+        device_id=at(side),
+        device_id_type=MESH,
+    )
+    chip_copy.start()
+    for k in range(head_chunks, chunks):
+        send_far(k)
+    own = chip[0:4] + over_groups(1)[0:4]
+    sums[1, 0:4, :] = own
+    own_copy = pltpu.make_async_remote_copy(
+        src_ref=sums.at[1],
+        dst_ref=sums.at[0],
+        send_sem=sums_send.at[0],
+        recv_sem=sums_recv.at[0],
+        device_id=at(-side),
+        device_id_type=MESH,
+    )
+    own_copy.start()
 
     cos = [tab_ref[pl.ds(COS + m * SUB, SUB), :] for m in range(quads)]
     sin = [tab_ref[pl.ds(SIN + m * SUB, SUB), :] for m in range(quads)]
@@ -296,8 +329,8 @@
             rtab[c, pl.ds(q * SUB, SUB), :] = sea_c / (1.0 + f2 * damp_c)
         return CURRENT_TOP * jnp.tanh(mean_x), CURRENT_TOP * jnp.tanh(mean_y), sea_c
 
-    flow_x, flow_y, _ = column(1, both)
-    sums_copies[1].wait_recv()
+    flow_x, flow_y, _ = column(1, own)
+    own_copy.wait_recv()
     flow_near, _, _ = column(0, sums[0])
     wide = (SUB, LANES)
     sign = side.astype(F32)
@@ -360,8 +393,8 @@
     )
     partial_copy.start()
 
-    sums_copies[0].wait_recv()
-    flow_far, _, sea_far = column(2, sums[2])
+    chip_copy.wait_recv()
+    flow_far, _, sea_far = column(2, sums[2, 0:4, :] + chip[4:8])
     face_far = jnp.broadcast_to(sign * (0.5 * (flow_x + flow_far)), wide)
 
     def far_level(l, acc):
@@ -397,7 +430,7 @@
     full_copy.start()
     partial_copy.wait_recv()
     last[...] = drift[2] + sea_far * shared
-    for copy in part_copies + link_copies + sums_copies + far_copies + [near_copy, partial_copy]:
+    for copy in part_copies + link_copies + far_copies + [near_copy, chip_copy, own_copy, partial_copy]:
         copy.wait_send()
     full_copy.wait()
     drift_ref[0] = drift[0]
@@ -435,12 +468,12 @@
     levels = bins // NDIR
     cells = currents.shape[2]
     table, padded = bin_tables(levels)
-    chunks = 6
+    chunks, head_chunks = 6, 4
     vmem = pl.BlockSpec(memory_space=pltpu.VMEM)
     hbm = pl.BlockSpec(memory_space=pltpu.HBM)
     dma = pltpu.SemaphoreType.DMA
     updated, drift, where = pl.pallas_call(
-        functools.partial(kernel, n_grp, n_dev, levels, padded, chunks),
+        functools.partial(kernel, n_grp, n_dev, levels, padded, chunks, head_chunks),
         out_shape=(
             jax.ShapeDtypeStruct((bins, width), F32),
             jax.ShapeDtypeStruct((3, SUB, width), F32),
@@ -458,17 +491,17 @@
             pltpu.VMEM((bins, width), F32),
             pltpu.VMEM((bins, width), F32),
             pltpu.VMEM((2, bins, width), F32),
-            pltpu.VMEM((n_grp, SUB, width), F32),
+            pltpu.VMEM((2, n_grp, SUB, width), F32),
             pltpu.VMEM((3, 3 * SUB, width), F32),
-            pltpu.VMEM((3, SUB, width), F32),
+            pltpu.VMEM((4, SUB, width), F32),
             pltpu.VMEM((4, SUB, width), F32),
             pltpu.VMEM((SUB, width), F32),
             pltpu.VMEM((3, padded, width), F32),
             dma((6,)),
             dma((chunks + 1,)),
             dma((chunks + 1,)),
-            dma((n_grp,)),
-            dma((n_grp,)),
+            dma((2, n_grp)),
+            dma((2, n_grp)),
             dma((2,)),
             dma((2,)),
             dma((2,)),

time: 28 us -> 26.8 us (0.957)
  Pallas kernels: 27.2 us -> 26 us
    pallas_call x1, Pallas kernels: 26.4 us -> 25.1 us  [body(): pl.pallas_call(functools.partial(kernel, n_grp, n_dev, levels, padded, ch...]
where the time goes in v6:
time: 26.8 us; the launch traced here: 26.6 us
  Pallas kernels  26 us (97%)
  between operations  0.64 us (2%)
    pallas_call x1, Pallas kernels, body(): pl.pallas_call(functools.partial(kernel, n_grp, n_dev, levels, padded, ch...  25.1 us
    pallas_call x1, Pallas kernels, body(): pl.pallas_call(finish, out_shape=(jax.ShapeDtypeStruct((bins, width), F32...  0.84 us

profile of v6, /device:TPU:1, one launch (start us, length us, event | category | flops | bytes accessed | tf_op | source)
XLA Modules:
  0.0 26.6 jit_solution(13390720432003188882)
XLA Ops:
  0.6 25.1 %wave_step.1 = (f32[1152,128]{1,0:T(8,128)S(1)}, f32[3,8,128]{2,1,0:T(8,128)S(1)}, s32[2,512]{1,0:T(2,128)S(1)}) custom-call(f32[1152,128]{1,0:T(8,128)} %bitcast.7, s32[1,128]{1,0:T(1,128)} %mask_hbm.1, f32[2,128]{1,0:T(2,128)} %bitcast.9, f32[2,512]{1,0:T(2,128)} %bitcast.8, s32[1,512]{1,0:T(1,128)} %coup_hbm.1, f32[224,128]{1,0:T(8,128)} %constant.2.clone.tab_hbm), custom_call_target="tpu_custom_call" | custom-call | tf_op jit(solution)/shard_map/wave_step/pallas_call | solution.py:475
  25.8 0.8 %finish.1 = (f32[1152,128]{1,0:T(8,128)}, f32[2,512]{1,0:T(2,128)}) custom-call(f32[1152,128]{1,0:T(8,128)S(1)} %get-tuple-element.7.upd_ref, f32[3,8,128]{2,1,0:T(8,128)S(1)} %get-tuple-element.8.drift, s32[2,512]{1,0:T(2,128)S(1)} %get-tuple-element.9.where_ref), custom_call_target="tpu_custom_call" | custom-call | tf_op jit(solution)/shard_map/finish/pallas_call | solution.py:529

commit v7 on v6

--- a/solution.py
+++ b/solution.py
@@ -63,8 +63,7 @@
     n_dev,
     levels,
     padded,
-    chunks,
-    head_chunks,
+    shared_levels,
     spec_hbm,
     mask_hbm,
     wind_hbm,
@@ -92,6 +91,8 @@
     load_sem,
     halo_send,
     halo_recv,
+    pass_send,
+    pass_recv,
     part_send,
     part_recv,
     link_send,
@@ -106,8 +107,6 @@
     side = 2 * lax.rem(d, 2) - 1
 
     bins = levels * NDIR
-    per = levels // chunks
-    rows = per * NDIR
     quads = NDIR // SUB
     COS, SIN, FG = 0, NDIR, 2 * NDIR
     F2, GS, WT = FG + padded, FG + 2 * padded, FG + 3 * padded
@@ -217,12 +216,22 @@
 
     link_copies = to_sides(link, link_send, link_recv)
 
+    half = shared_levels // 2
+    parity = lax.rem(g, 2)
+    mine, theirs = parity * shared_levels, (1 - parity) * shared_levels
+    first, middle = 2 * shared_levels, 28
+    spans = ((mine, half), (mine + half, half), (first, middle - first), (middle, levels - middle))
+
+    def span(start, count):
+        return pl.ds(pl.multiple_of(start * NDIR, NDIR), count * NDIR)
+
     far_copies = []
 
     def send_far(k):
+        there = span(*spans[k])
         copy = pltpu.make_async_remote_copy(
-            src_ref=ctr.at[pl.ds(k * rows, rows), :],
-            dst_ref=far.at[pl.ds(k * rows, rows), :],
+            src_ref=ctr.at[there, :],
+            dst_ref=far.at[there, :],
             send_sem=halo_send.at[k],
             recv_sem=halo_recv.at[k],
             device_id=at(side),
@@ -269,14 +278,19 @@
     near_copy = pltpu.make_async_remote_copy(
         src_ref=ctr,
         dst_ref=near,
-        send_sem=halo_send.at[chunks],
-        recv_sem=halo_recv.at[chunks],
+        send_sem=halo_send.at[4],
+        recv_sem=halo_recv.at[4],
         device_id=at(-side),
         device_id_type=MESH,
     )
     near_copy.start()
-    for k in range(1, head_chunks):
-        send_far(k)
+    send_far(1)
+    send_far(2)
+
+    def damping(c, sea_c, damp_c):
+        for q in range(padded // SUB):
+            f2 = tab_ref[pl.ds(F2 + q * SUB, SUB), :]
+            rtab[c, pl.ds(q * SUB, SUB), :] = sea_c / (1.0 + f2 * damp_c)
 
     link_copies[1].wait_recv()
     part[0, g, 0:4, :] = cell_sums[4:8] + pick(link[0], 8, 0)
@@ -285,6 +299,9 @@
     link_copies[0].wait_recv()
     part[1, g, 0:4, :] = pick(link[2], 0, 8)
     part_copies += to_groups(1)
+    damping(1, sea, damp)
+    for c in (0, 2):
+        damping(c, link[c, 2 * SUB : 2 * SUB + 1, :], link[c, 2 * SUB + 1 : 2 * SUB + 2, :])
     chip = over_groups(0)
     sums[3] = chip
     chip_copy = pltpu.make_async_remote_copy(
@@ -296,8 +313,21 @@
         device_id_type=MESH,
     )
     chip_copy.start()
-    for k in range(head_chunks, chunks):
-        send_far(k)
+    send_far(3)
+    pass_copies = []
+    for i, step in ((0, 1), (1, n_grp - 1)):
+        far_copies[i].wait_recv()
+        there = span(*spans[i])
+        copy = pltpu.make_async_remote_copy(
+            src_ref=far.at[there, :],
+            dst_ref=far.at[there, :],
+            send_sem=pass_send.at[i],
+            recv_sem=pass_recv.at[i],
+            device_id=group(step),
+            device_id_type=MESH,
+        )
+        copy.start()
+        pass_copies.append(copy)
     own = chip[0:4] + over_groups(1)[0:4]
     sums[1, 0:4, :] = own
     own_copy = pltpu.make_async_remote_copy(
@@ -320,13 +350,9 @@
         mean_y = s4[1:2] / count
         row = 2 * SUB
         sea_c = link[c, row : row + 1, :]
-        damp_c = link[c, row + 1 : row + 2, :]
         wx = link[c, row + 2 : row + 3, :] - mean_x
         wy = link[c, row + 3 : row + 4, :] - mean_y
         gain[c] = [cos[m] * wx + sin[m] * wy for m in range(quads)]
-        for q in range(padded // SUB):
-            f2 = tab_ref[pl.ds(F2 + q * SUB, SUB), :]
-            rtab[c, pl.ds(q * SUB, SUB), :] = sea_c / (1.0 + f2 * damp_c)
         return CURRENT_TOP * jnp.tanh(mean_x), CURRENT_TOP * jnp.tanh(mean_y), sea_c
 
     flow_x, flow_y, _ = column(1, own)
@@ -413,9 +439,25 @@
         return tuple(out)
 
     acc = (zero,) * quads
-    for k in range(chunks):
+
+    def far_levels(start, count, acc):
+        return lax.fori_loop(0, count, lambda i, acc: far_level(start + i, acc), acc, unroll=4)
+
+    acc = far_levels(mine, shared_levels, acc)
+    for k in (2, 3):
         far_copies[k].wait_recv()
-        acc = lax.fori_loop(k * per, (k + 1) * per, far_level, acc, unroll=per)
+        acc = far_levels(*spans[k], acc)
+    for i in range(2):
+        here = span(theirs + i * half, half)
+        pltpu.make_async_remote_copy(
+            src_ref=far.at[here, :],
+            dst_ref=far.at[here, :],
+            send_sem=pass_send.at[i],
+            recv_sem=pass_recv.at[i],
+            device_id=group(1 + i * (n_grp - 2)),
+            device_id_type=MESH,
+        ).wait_recv()
+    acc = far_levels(theirs, shared_levels, acc)
 
     shared = drift_rows(acc)
     drift[1] = drift[3] - sea * shared
@@ -430,7 +472,7 @@
     full_copy.start()
     partial_copy.wait_recv()
     last[...] = drift[2] + sea_far * shared
-    for copy in part_copies + link_copies + far_copies + [near_copy, chip_copy, own_copy, partial_copy]:
+    for copy in part_copies + link_copies + far_copies + pass_copies + [near_copy, chip_copy, own_copy, partial_copy]:
         copy.wait_send()
     full_copy.wait()
     drift_ref[0] = drift[0]
@@ -468,12 +510,12 @@
     levels = bins // NDIR
     cells = currents.shape[2]
     table, padded = bin_tables(levels)
-    chunks, head_chunks = 6, 4
+    shared_levels = 8
     vmem = pl.BlockSpec(memory_space=pltpu.VMEM)
     hbm = pl.BlockSpec(memory_space=pltpu.HBM)
     dma = pltpu.SemaphoreType.DMA
     updated, drift, where = pl.pallas_call(
-        functools.partial(kernel, n_grp, n_dev, levels, padded, chunks, head_chunks),
+        functools.partial(kernel, n_grp, n_dev, levels, padded, shared_levels),
         out_shape=(
             jax.ShapeDtypeStruct((bins, width), F32),
             jax.ShapeDtypeStruct((3, SUB, width), F32),
@@ -498,8 +540,10 @@
             pltpu.VMEM((SUB, width), F32),
             pltpu.VMEM((3, padded, width), F32),
             dma((6,)),
-            dma((chunks + 1,)),
-            dma((chunks + 1,)),
+            dma((5,)),
+            dma((5,)),
+            dma((2,)),
+            dma((2,)),
             dma((2, n_grp)),
             dma((2, n_grp)),
             dma((2,)),

time: 26.8 us -> 25.7 us (0.959)
  Pallas kernels: 26 us -> 25 us
    pallas_call x1, Pallas kernels: 25.1 us -> 24.1 us  [body(): pl.pallas_call(functools.partial(kernel, n_grp, n_dev, levels, padded, sh...]
where the time goes in v7:
time: 25.7 us; the launch traced here: 25.6 us
  Pallas kernels  25 us (97%)
  between operations  0.64 us (2%)
    pallas_call x1, Pallas kernels, body(): pl.pallas_call(functools.partial(kernel, n_grp, n_dev, levels, padded, sh...  24.1 us
    pallas_call x1, Pallas kernels, body(): pl.pallas_call(finish, out_shape=(jax.ShapeDtypeStruct((bins, width), F32...  0.84 us

profile of v7, /device:TPU:1, one launch (start us, length us, event | category | flops | bytes accessed | tf_op | source)
XLA Modules:
  0.0 25.6 jit_solution(6906035552222642068)
XLA Ops:
  0.6 24.1 %wave_step.1 = (f32[1152,128]{1,0:T(8,128)S(1)}, f32[3,8,128]{2,1,0:T(8,128)S(1)}, s32[2,512]{1,0:T(2,128)S(1)}) custom-call(f32[1152,128]{1,0:T(8,128)} %bitcast.7, s32[1,128]{1,0:T(1,128)} %mask_hbm.1, f32[2,128]{1,0:T(2,128)} %bitcast.9, f32[2,512]{1,0:T(2,128)} %bitcast.8, s32[1,512]{1,0:T(1,128)} %coup_hbm.1, f32[224,128]{1,0:T(8,128)} %constant.2.clone.tab_hbm), custom_call_target="tpu_custom_call" | custom-call | tf_op jit(solution)/shard_map/wave_step/pallas_call | solution.py:517
  24.8 0.8 %finish.1 = (f32[1152,128]{1,0:T(8,128)}, f32[2,512]{1,0:T(2,128)}) custom-call(f32[1152,128]{1,0:T(8,128)S(1)} %get-tuple-element.7.upd_ref, f32[3,8,128]{2,1,0:T(8,128)S(1)} %get-tuple-element.8.drift, s32[2,512]{1,0:T(2,128)S(1)} %get-tuple-element.9.where_ref), custom_call_target="tpu_custom_call" | custom-call | tf_op jit(solution)/shard_map/finish/pallas_call | solution.py:573

commit v8 on v7

--- a/solution.py
+++ b/solution.py
@@ -82,6 +82,7 @@
     near,
     far,
     base,
+    speed,
     part,
     link,
     sums,
@@ -95,6 +96,7 @@
     pass_recv,
     part_send,
     part_recv,
+    share_send,
     link_send,
     link_recv,
     sums_send,
@@ -133,10 +135,16 @@
     for load in loads:
         load.start()
     barrier = pltpu.get_barrier_semaphore()
-    for k in range(1, n_grp):
-        pl.semaphore_signal(barrier, inc=1, device_id=group(k), device_id_type=MESH)
-    for step in (-side, side):
-        pl.semaphore_signal(barrier, inc=1, device_id=at(step), device_id_type=MESH)
+    for peer in [at(side), at(-side)] + [group(k) for k in range(1, n_grp)]:
+        pl.semaphore_signal(barrier, inc=1, device_id=peer, device_id_type=MESH)
+
+    def across(step):
+        return {"grp": lax.rem(g + step, n_grp), "dev": lax.rem(d + side + n_dev, n_dev)}
+
+    @pl.when(side < 0)
+    def _():
+        for k in range(1, n_grp):
+            pl.semaphore_signal(barrier, inc=1, device_id=across(k), device_id_type=MESH)
 
     loads[0].wait()
     loads[1].wait()
@@ -158,7 +166,8 @@
             split3(value), one_hot, (((1,), (1,)), ((), ())), preferred_element_type=F32
         )
     )
-    link[1, 0 : 2 * SUB, :] = cell_sums
+    link[1, 0:4, :] = jnp.where(side > 0, cell_sums[8:12], cell_sums[0:4])
+    link[3, 0:4, :] = jnp.where(side > 0, cell_sums[0:4], cell_sums[8:12])
     part[1, g] = jnp.zeros((SUB, LANES), F32)
     sums[1] = jnp.zeros((SUB, LANES), F32)
     where_ref[0:1, :] = jnp.where(g > 0, 1 + (slot - 1) * side, 3)
@@ -187,39 +196,74 @@
     steepness = STEEP_SCALE * total * mean_freq**4
     damp = WHITECAP * (steepness / mean_freq) ** 2
     which = lax.broadcasted_iota(jnp.int32, (SUB, LANES), 0)
-    link[1, 2 * SUB :, :] = jnp.where(
-        which == 0,
-        sea,
-        jnp.where(
-            which == 1,
-            damp,
-            jnp.where(which == 2, wind_ref[0:1, :], jnp.where(which == 3, wind_ref[1:2, :], 0.0)),
-        ),
-    )
-
-    pl.semaphore_wait(barrier, n_grp - 1 + 2)
-
-    def to_sides(buf, send_sem, recv_sem):
-        copies = []
-        for i, step in ((1, side), (0, -side)):
-            copy = pltpu.make_async_remote_copy(
-                src_ref=buf.at[1],
-                dst_ref=buf.at[2 * i],
-                send_sem=send_sem.at[i],
-                recv_sem=recv_sem.at[i],
-                device_id=at(step),
-                device_id_type=MESH,
-            )
-            copy.start()
-            copies.append(copy)
-        return copies
-
-    link_copies = to_sides(link, link_send, link_recv)
+    for i in (1, 3):
+        for n, term in enumerate((sea, damp, wind_ref[0:1, :], wind_ref[1:2, :])):
+            link[i, 4 + n : 5 + n, :] = term
+
+    def damping(c, sea_c, damp_c):
+        for q in range(padded // SUB):
+            f2 = tab_ref[pl.ds(F2 + q * SUB, SUB), :]
+            rtab[c, pl.ds(q * SUB, SUB), :] = sea_c / (1.0 + f2 * damp_c)
+
+    damping(1, sea, damp)
+    wide = (SUB, LANES)
+    sign = side.astype(F32)
+    cos = [tab_ref[pl.ds(COS + m * SUB, SUB), :] for m in range(quads)]
+    sin = [tab_ref[pl.ds(SIN + m * SUB, SUB), :] for m in range(quads)]
+    lane = lax.broadcasted_iota(jnp.int32, wide, 1)
+    has_n = lane < LANES - 1
+    has_s = lane > 0
+    away = [sign * cos[m] for m in range(quads)]
+
+    def speed_level(l, carry):
+        gs = tab_ref[pl.ds(GS + l, 1), :]
+        rec = rtab[1, pl.ds(l, 1), :]
+        for m in range(quads):
+            r = pl.ds(pl.multiple_of(l * NDIR + m * SUB, SUB), SUB)
+            y = gs * sin[m]
+            speed[0, r, :] = jnp.where(has_n, y, 0.0)
+            speed[1, r, :] = jnp.where(has_s, y, 0.0)
+            speed[2, r, :] = gs * away[m]
+            base[0, r, :] = ctr[r, :] * rec
+        return carry
+
+    lax.fori_loop(0, levels, speed_level, 0, unroll=4)
+
+    pl.semaphore_wait(barrier, n_grp + 1 + jnp.where(side > 0, n_grp - 1, 0))
+
+    link_copies = []
+    for i, step in ((1, side), (0, -side)):
+        copy = pltpu.make_async_remote_copy(
+            src_ref=link.at[3 - 2 * i],
+            dst_ref=link.at[2 * i],
+            send_sem=link_send.at[i],
+            recv_sem=link_recv.at[i],
+            device_id=at(step),
+            device_id_type=MESH,
+        )
+        copy.start()
+        link_copies.append(copy)
+
+    def share_copy(k):
+        return pltpu.make_async_remote_copy(
+            src_ref=link.at[1],
+            dst_ref=part.at[1, g],
+            send_sem=share_send.at[k],
+            recv_sem=part_recv.at[1, g],
+            device_id=across(k),
+            device_id_type=MESH,
+        )
+
+    @pl.when(side > 0)
+    def _():
+        for k in range(1, n_grp):
+            share_copy(k).start()
+
 
     half = shared_levels // 2
     parity = lax.rem(g, 2)
     mine, theirs = parity * shared_levels, (1 - parity) * shared_levels
-    first, middle = 2 * shared_levels, 28
+    first, middle = 2 * shared_levels, 32
     spans = ((mine, half), (mine + half, half), (first, middle - first), (middle, levels - middle))
 
     def span(start, count):
@@ -240,23 +284,15 @@
         copy.start()
         far_copies.append(copy)
 
-    def pick(buf, east, west):
-        return jnp.where(side > 0, buf[east : east + 4], buf[west : west + 4])
-
-    def to_groups(n):
-        copies = []
-        for k in range(1, n_grp):
-            copy = pltpu.make_async_remote_copy(
-                src_ref=part.at[n, g],
-                dst_ref=part.at[n, g],
-                send_sem=part_send.at[n, k],
-                recv_sem=part_recv.at[n, g],
-                device_id=group(k),
-                device_id_type=MESH,
-            )
-            copy.start()
-            copies.append(copy)
-        return copies
+    def group_copy(n, k):
+        return pltpu.make_async_remote_copy(
+            src_ref=part.at[n, g],
+            dst_ref=part.at[n, g],
+            send_sem=part_send.at[n, k],
+            recv_sem=part_recv.at[n, g],
+            device_id=group(k),
+            device_id_type=MESH,
+        )
 
     def over_groups(n):
         for k in range(1, n_grp):
@@ -287,21 +323,31 @@
     send_far(1)
     send_far(2)
 
-    def damping(c, sea_c, damp_c):
-        for q in range(padded // SUB):
-            f2 = tab_ref[pl.ds(F2 + q * SUB, SUB), :]
-            rtab[c, pl.ds(q * SUB, SUB), :] = sea_c / (1.0 + f2 * damp_c)
-
     link_copies[1].wait_recv()
-    part[0, g, 0:4, :] = cell_sums[4:8] + pick(link[0], 8, 0)
-    part[0, g, 4:8, :] = pick(cell_sums, 8, 0)
-    part_copies = to_groups(0)
+    part[0, g, 0:4, :] = cell_sums[4:8] + link[0, 0:4, :]
+    part[0, g, 4:8, :] = link[1, 0:4, :]
+    for k in range(1, n_grp):
+        group_copy(0, k).start()
     link_copies[0].wait_recv()
-    part[1, g, 0:4, :] = pick(link[2], 0, 8)
-    part_copies += to_groups(1)
-    damping(1, sea, damp)
+    part[1, g, 0:4, :] = link[2, 0:4, :]
+
+    @pl.when(side > 0)
+    def _():
+        for k in range(1, n_grp):
+            group_copy(1, k).start()
+
     for c in (0, 2):
-        damping(c, link[c, 2 * SUB : 2 * SUB + 1, :], link[c, 2 * SUB + 1 : 2 * SUB + 2, :])
+        damping(c, link[c, 4:5, :], link[c, 5:6, :])
+    near_copy.wait_recv()
+
+    def near_level(l, carry):
+        rec = rtab[0, pl.ds(l, 1), :]
+        for m in range(quads):
+            r = pl.ds(pl.multiple_of(l * NDIR + m * SUB, SUB), SUB)
+            base[1, r, :] = near[r, :] * rec
+        return carry
+
+    lax.fori_loop(0, levels, near_level, 0, unroll=6)
     chip = over_groups(0)
     sums[3] = chip
     chip_copy = pltpu.make_async_remote_copy(
@@ -340,38 +386,29 @@
     )
     own_copy.start()
 
-    cos = [tab_ref[pl.ds(COS + m * SUB, SUB), :] for m in range(quads)]
-    sin = [tab_ref[pl.ds(SIN + m * SUB, SUB), :] for m in range(quads)]
     gain = {}
 
     def column(c, s4):
         count = jnp.maximum(s4[2:3], 1.0)
         mean_x = s4[0:1] / count
         mean_y = s4[1:2] / count
-        row = 2 * SUB
-        sea_c = link[c, row : row + 1, :]
-        wx = link[c, row + 2 : row + 3, :] - mean_x
-        wy = link[c, row + 3 : row + 4, :] - mean_y
+        sea_c = link[c, 4:5, :]
+        wx = link[c, 6:7, :] - mean_x
+        wy = link[c, 7:8, :] - mean_y
         gain[c] = [cos[m] * wx + sin[m] * wy for m in range(quads)]
         return CURRENT_TOP * jnp.tanh(mean_x), CURRENT_TOP * jnp.tanh(mean_y), sea_c
 
     flow_x, flow_y, _ = column(1, own)
     own_copy.wait_recv()
     flow_near, _, _ = column(0, sums[0])
-    wide = (SUB, LANES)
-    sign = side.astype(F32)
     face_near = jnp.broadcast_to(-sign * (0.5 * (flow_near + flow_x)), wide)
     flow_y = jnp.broadcast_to(flow_y, wide)
-    face_n = 0.5 * (flow_y + pltpu.roll(flow_y, LANES - 1, 1))
-    face_s = 0.5 * (flow_y + pltpu.roll(flow_y, 1, 1))
+    face_n = jnp.where(has_n, 0.5 * (flow_y + pltpu.roll(flow_y, LANES - 1, 1)), 0.0)
+    face_s = jnp.where(has_s, 0.5 * (flow_y + pltpu.roll(flow_y, 1, 1)), 0.0)
     sea_w = jnp.broadcast_to(sea, wide)
-    lane = lax.broadcasted_iota(jnp.int32, wide, 1)
-    has_n = lane < LANES - 1
-    has_s = lane > 0
-    away = [sign * cos[m] for m in range(quads)]
-
-    def forced(energy, c, m, fg, rec):
-        return energy * (jnp.maximum(gain[c][m] * fg + (1.0 - WIND_GAIN), 1.0) * rec)
+
+    def forced(damped, c, m, fg):
+        return damped * jnp.maximum(gain[c][m] * fg + (1.0 - WIND_GAIN), 1.0)
 
     def drift_rows(acc):
         dx = acc[0] * cos[0]
@@ -385,19 +422,15 @@
 
     def own_level(l, acc):
         fg = tab_ref[pl.ds(FG + l, 1), :]
-        gs = tab_ref[pl.ds(GS + l, 1), :]
         wt = tab_ref[pl.ds(WT + l, 1), :]
-        rec = rtab[1, pl.ds(l, 1), :]
-        rec_near = rtab[0, pl.ds(l, 1), :]
         out = []
         for m in range(quads):
             r = pl.ds(pl.multiple_of(l * NDIR + m * SUB, SUB), SUB)
-            e = forced(ctr[r, :], 1, m, fg, rec)
-            other = forced(near[r, :], 0, m, fg, rec_near)
-            speed = gs * sin[m]
-            a = jnp.where(has_n, speed + face_n, 0.0)
-            b = jnp.where(has_s, speed + face_s, 0.0)
-            c = face_near - gs * away[m]
+            e = forced(base[0, r, :], 1, m, fg)
+            other = forced(base[1, r, :], 0, m, fg)
+            a = speed[0, r, :] + face_n
+            b = speed[1, r, :] + face_s
+            c = face_near - speed[2, r, :]
             flux_n = a * jnp.where(a > 0.0, e, pltpu.roll(e, LANES - 1, 1))
             flux_s = b * jnp.where(b > 0.0, pltpu.roll(e, 1, 1), e)
             u = sea_w * (e - flux_n + flux_s - c * jnp.where(c > 0.0, e, other))
@@ -406,7 +439,6 @@
             out.append(acc[m] + wt * u)
         return tuple(out)
 
-    near_copy.wait_recv()
     acc = lax.fori_loop(0, levels, own_level, (zero,) * quads, unroll=6)
     drift[3] = drift_rows(acc)
     partial_copy = pltpu.make_async_remote_copy(
@@ -425,14 +457,13 @@
 
     def far_level(l, acc):
         fg = tab_ref[pl.ds(FG + l, 1), :]
-        gs = tab_ref[pl.ds(GS + l, 1), :]
         wt = tab_ref[pl.ds(WT + l, 1), :]
         rec = rtab[2, pl.ds(l, 1), :]
         out = []
         for m in range(quads):
             r = pl.ds(pl.multiple_of(l * NDIR + m * SUB, SUB), SUB)
-            other = forced(far[r, :], 2, m, fg, rec)
-            a = gs * away[m] + face_far
+            other = forced(far[r, :] * rec, 2, m, fg)
+            a = speed[2, r, :] + face_far
             flux = a * jnp.where(a > 0.0, base[0, r, :], other)
             upd_ref[r, :] = base[1, r, :] - sea_w * flux
             out.append(acc[m] + wt * flux)
@@ -472,7 +503,16 @@
     full_copy.start()
     partial_copy.wait_recv()
     last[...] = drift[2] + sea_far * shared
-    for copy in part_copies + link_copies + far_copies + pass_copies + [near_copy, chip_copy, own_copy, partial_copy]:
+    for k in range(1, n_grp):
+        group_copy(0, k).wait_send()
+
+    @pl.when(side > 0)
+    def _():
+        for k in range(1, n_grp):
+            group_copy(1, k).wait_send()
+            share_copy(k).wait_send()
+
+    for copy in link_copies + far_copies + pass_copies + [near_copy, chip_copy, own_copy, partial_copy]:
         copy.wait_send()
     full_copy.wait()
     drift_ref[0] = drift[0]
@@ -483,22 +523,15 @@
 def finish(upd_ref, drift, where_ref, upd_hbm, cell_hbm, cell_ref, sem):
     store = pltpu.make_async_copy(upd_ref, upd_hbm, sem.at[0])
     store.start()
-    slot = where_ref[0:1, :]
-    row = where_ref[1:2, :]
-    cells = row.shape[1]
-    one_hot = jnp.where(
-        lax.broadcasted_iota(jnp.int32, (LANES, cells), 0) == row, 1.0, 0.0
-    ).astype(BF16)
-    band = jnp.zeros((2 * SUB, LANES), F32)
-    place = lax.broadcasted_iota(jnp.int32, (2 * SUB, LANES), 0)
-    for c in range(3):
-        for v in range(2):
-            band = jnp.where(place == 4 * c + v, drift[c, v : v + 1, :], band)
-    picked = sum3(jnp.dot(split3(band), one_hot, preferred_element_type=F32))
-    for v in range(2):
-        out = jnp.where(slot == 2, picked[8 + v : 9 + v], 0.0)
-        out = jnp.where(slot == 1, picked[4 + v : 5 + v], out)
-        cell_ref[v : v + 1, :] = jnp.where(slot == 0, picked[v : v + 1], out)
+    cells = where_ref.shape[1]
+    for j in range(cells // LANES):
+        here = pl.ds(j * LANES, LANES)
+        role = where_ref[0:1, here]
+        row = jnp.broadcast_to(where_ref[1:2, here], (SUB, LANES))
+        out = jnp.zeros((SUB, LANES), F32)
+        for c in range(3):
+            out = jnp.where(role == c, jnp.take_along_axis(drift[c], row, axis=1), out)
+        cell_ref[:, here] = out[0:2]
     cell_store = pltpu.make_async_copy(cell_ref, cell_hbm, sem.at[1])
     cell_store.start()
     cell_store.wait()
@@ -533,8 +566,9 @@
             pltpu.VMEM((bins, width), F32),
             pltpu.VMEM((bins, width), F32),
             pltpu.VMEM((2, bins, width), F32),
+            pltpu.VMEM((3, bins, width), F32),
             pltpu.VMEM((2, n_grp, SUB, width), F32),
-            pltpu.VMEM((3, 3 * SUB, width), F32),
+            pltpu.VMEM((4, SUB, width), F32),
             pltpu.VMEM((4, SUB, width), F32),
             pltpu.VMEM((4, SUB, width), F32),
             pltpu.VMEM((SUB, width), F32),
@@ -546,6 +580,7 @@
             dma((2,)),
             dma((2, n_grp)),
             dma((2, n_grp)),
+            dma((n_grp,)),
             dma((2,)),
             dma((2,)),
             dma((2,)),

time: 25.7 us -> 25.6 us (level)
  the two profiles are of different devices: /device:TPU:1 before, /device:TPU:8 now
where the time goes in v8:
time: 25.6 us; the launch traced here: 25.4 us
  Pallas kernels  24.8 us (97%)
  between operations  0.64 us (2%)
    pallas_call x1, Pallas kernels, body(): pl.pallas_call(functools.partial(kernel, n_grp, n_dev, levels, padded, sh...  23.9 us
    pallas_call x1, Pallas kernels, body(): pl.pallas_call(finish, out_shape=(jax.ShapeDtypeStruct((bins, width), F32...  0.84 us

profile of v8, /device:TPU:8, one launch (start us, length us, event | category | flops | bytes accessed | tf_op | source)
XLA Modules:
  0.0 25.4 jit_solution(11457585175699197279)
XLA Ops:
  0.6 23.9 %wave_step.1 = (f32[1152,128]{1,0:T(8,128)S(1)}, f32[3,8,128]{2,1,0:T(8,128)S(1)}, s32[2,512]{1,0:T(2,128)S(1)}) custom-call(f32[1152,128]{1,0:T(8,128)} %bitcast.7, s32[1,128]{1,0:T(1,128)} %mask_hbm.1, f32[2,128]{1,0:T(2,128)} %bitcast.9, f32[2,512]{1,0:T(2,128)} %bitcast.8, s32[1,512]{1,0:T(1,128)} %coup_hbm.1, f32[224,128]{1,0:T(8,128)} %constant.2.clone.tab_hbm), custom_call_target="tpu_custom_call" | custom-call | tf_op jit(solution)/shard_map/wave_step/pallas_call | solution.py:550
  24.6 0.8 %finish.1 = (f32[1152,128]{1,0:T(8,128)}, f32[2,512]{1,0:T(2,128)}) custom-call(f32[1152,128]{1,0:T(8,128)S(1)} %get-tuple-element.7.upd_ref, f32[3,8,128]{2,1,0:T(8,128)S(1)} %get-tuple-element.8.drift, s32[2,512]{1,0:T(2,128)S(1)} %get-tuple-element.9.where_ref), custom_call_target="tpu_custom_call" | custom-call | tf_op jit(solution)/shard_map/finish/pallas_call | solution.py:608

commit v9 on v8

--- a/solution.py
+++ b/solution.py
@@ -254,7 +254,7 @@
             device_id_type=MESH,
         )
 
-    @pl.when(side > 0)
+    @pl.when(jnp.logical_and(side > 0, g > 0))
     def _():
         for k in range(1, n_grp):
             share_copy(k).start()
@@ -295,16 +295,19 @@
         )
 
     def over_groups(n):
-        for k in range(1, n_grp):
-            src = lax.rem(g - k + n_grp, n_grp)
-            pltpu.make_async_remote_copy(
-                src_ref=part.at[n, src],
-                dst_ref=part.at[n, src],
-                send_sem=part_send.at[n, k],
-                recv_sem=part_recv.at[n, src],
-                device_id=group(k),
-                device_id_type=MESH,
-            ).wait_recv()
+        for src in range(1, n_grp):
+
+            @pl.when(g != src)
+            def _(src=src):
+                pltpu.make_async_remote_copy(
+                    src_ref=part.at[n, src],
+                    dst_ref=part.at[n, src],
+                    send_sem=part_send.at[n, 1],
+                    recv_sem=part_recv.at[n, src],
+                    device_id=group(1),
+                    device_id_type=MESH,
+                ).wait_recv()
+
         both = part[n, 1]
         for k in range(2, n_grp):
             both = both + part[n, k]
@@ -326,12 +329,16 @@
     link_copies[1].wait_recv()
     part[0, g, 0:4, :] = cell_sums[4:8] + link[0, 0:4, :]
     part[0, g, 4:8, :] = link[1, 0:4, :]
-    for k in range(1, n_grp):
-        group_copy(0, k).start()
+
+    @pl.when(g > 0)
+    def _():
+        for k in range(1, n_grp):
+            group_copy(0, k).start()
+
     link_copies[0].wait_recv()
     part[1, g, 0:4, :] = link[2, 0:4, :]
 
-    @pl.when(side > 0)
+    @pl.when(jnp.logical_and(side > 0, g > 0))
     def _():
         for k in range(1, n_grp):
             group_copy(1, k).start()
@@ -503,10 +510,12 @@
     full_copy.start()
     partial_copy.wait_recv()
     last[...] = drift[2] + sea_far * shared
-    for k in range(1, n_grp):
-        group_copy(0, k).wait_send()
-
-    @pl.when(side > 0)
+    @pl.when(g > 0)
+    def _():
+        for k in range(1, n_grp):
+            group_copy(0, k).wait_send()
+
+    @pl.when(jnp.logical_and(side > 0, g > 0))
     def _():
         for k in range(1, n_grp):
             group_copy(1, k).wait_send()

time: 25.6 us -> 25.6 us (level)
  no operation moved by 1% of the time
where the time goes in v9:
time: 25.6 us; the launch traced here: 25.4 us
  Pallas kernels  24.8 us (97%)
  between operations  0.64 us (2%)
    pallas_call x1, Pallas kernels, body(): pl.pallas_call(functools.partial(kernel, n_grp, n_dev, levels, padded, sh...  23.9 us
    pallas_call x1, Pallas kernels, body(): pl.pallas_call(finish, out_shape=(jax.ShapeDtypeStruct((bins, width), F32...  0.84 us

profile of v9, /device:TPU:8, one launch (start us, length us, event | category | flops | bytes accessed | tf_op | source)
XLA Modules:
  0.0 25.4 jit_solution(5056580603831650330)
XLA Ops:
  0.6 23.9 %wave_step.1 = (f32[1152,128]{1,0:T(8,128)S(1)}, f32[3,8,128]{2,1,0:T(8,128)S(1)}, s32[2,512]{1,0:T(2,128)S(1)}) custom-call(f32[1152,128]{1,0:T(8,128)} %bitcast.7, s32[1,128]{1,0:T(1,128)} %mask_hbm.1, f32[2,128]{1,0:T(2,128)} %bitcast.9, f32[2,512]{1,0:T(2,128)} %bitcast.8, s32[1,512]{1,0:T(1,128)} %coup_hbm.1, f32[224,128]{1,0:T(8,128)} %constant.2.clone.tab_hbm), custom_call_target="tpu_custom_call" | custom-call | tf_op jit(solution)/shard_map/wave_step/pallas_call | solution.py:559
  24.6 0.8 %finish.1 = (f32[1152,128]{1,0:T(8,128)}, f32[2,512]{1,0:T(2,128)}) custom-call(f32[1152,128]{1,0:T(8,128)S(1)} %get-tuple-element.7.upd_ref, f32[3,8,128]{2,1,0:T(8,128)S(1)} %get-tuple-element.8.drift, s32[2,512]{1,0:T(2,128)S(1)} %get-tuple-element.9.where_ref), custom_call_target="tpu_custom_call" | custom-call | tf_op jit(solution)/shard_map/finish/pallas_call | solution.py:617

commit v10 on v9

--- a/solution.py
+++ b/solution.py
@@ -89,6 +89,7 @@
     drift,
     last,
     rtab,
+    near_flow,
     load_sem,
     halo_send,
     halo_recv,
@@ -381,6 +382,41 @@
         )
         copy.start()
         pass_copies.append(copy)
+    gain = {}
+
+    def column(c, s4):
+        count = jnp.maximum(s4[2:3], 1.0)
+        mean_x = s4[0:1] / count
+        mean_y = s4[1:2] / count
+        sea_c = link[c, 4:5, :]
+        wx = link[c, 6:7, :] - mean_x
+        wy = link[c, 7:8, :] - mean_y
+        gain[c] = [cos[m] * wx + sin[m] * wy for m in range(quads)]
+        return CURRENT_TOP * jnp.tanh(mean_x), CURRENT_TOP * jnp.tanh(mean_y), sea_c
+
+    def near_forced():
+        pltpu.make_async_remote_copy(
+            src_ref=sums.at[1],
+            dst_ref=sums.at[0],
+            send_sem=sums_send.at[0],
+            recv_sem=sums_recv.at[0],
+            device_id=at(-side),
+            device_id_type=MESH,
+        ).wait_recv()
+        near_flow[...] = jnp.broadcast_to(column(0, sums[0])[0], wide)
+
+        def level(l, carry):
+            fg = tab_ref[pl.ds(FG + l, 1), :]
+            for m in range(quads):
+                r = pl.ds(pl.multiple_of(l * NDIR + m * SUB, SUB), SUB)
+                base[1, r, :] = base[1, r, :] * jnp.maximum(
+                    gain[0][m] * fg + (1.0 - WIND_GAIN), 1.0
+                )
+            return carry
+
+        lax.fori_loop(0, levels, level, 0, unroll=6)
+
+    pl.when(side > 0)(near_forced)
     own = chip[0:4] + over_groups(1)[0:4]
     sums[1, 0:4, :] = own
     own_copy = pltpu.make_async_remote_copy(
@@ -393,22 +429,9 @@
     )
     own_copy.start()
 
-    gain = {}
-
-    def column(c, s4):
-        count = jnp.maximum(s4[2:3], 1.0)
-        mean_x = s4[0:1] / count
-        mean_y = s4[1:2] / count
-        sea_c = link[c, 4:5, :]
-        wx = link[c, 6:7, :] - mean_x
-        wy = link[c, 7:8, :] - mean_y
-        gain[c] = [cos[m] * wx + sin[m] * wy for m in range(quads)]
-        return CURRENT_TOP * jnp.tanh(mean_x), CURRENT_TOP * jnp.tanh(mean_y), sea_c
-
     flow_x, flow_y, _ = column(1, own)
-    own_copy.wait_recv()
-    flow_near, _, _ = column(0, sums[0])
-    face_near = jnp.broadcast_to(-sign * (0.5 * (flow_near + flow_x)), wide)
+    pl.when(side < 0)(near_forced)
+    face_near = jnp.broadcast_to(-sign * (0.5 * (near_flow[...] + flow_x)), wide)
     flow_y = jnp.broadcast_to(flow_y, wide)
     face_n = jnp.where(has_n, 0.5 * (flow_y + pltpu.roll(flow_y, LANES - 1, 1)), 0.0)
     face_s = jnp.where(has_s, 0.5 * (flow_y + pltpu.roll(flow_y, 1, 1)), 0.0)
@@ -434,7 +457,7 @@
         for m in range(quads):
             r = pl.ds(pl.multiple_of(l * NDIR + m * SUB, SUB), SUB)
             e = forced(base[0, r, :], 1, m, fg)
-            other = forced(base[1, r, :], 0, m, fg)
+            other = base[1, r, :]
             a = speed[0, r, :] + face_n
             b = speed[1, r, :] + face_s
             c = face_near - speed[2, r, :]
@@ -582,6 +605,7 @@
             pltpu.VMEM((4, SUB, width), F32),
             pltpu.VMEM((SUB, width), F32),
             pltpu.VMEM((3, padded, width), F32),
+            pltpu.VMEM((SUB, width), F32),
             dma((6,)),
             dma((5,)),
             dma((5,)),

time: 25.6 us -> 25.5 us (level)
  no operation moved by 1% of the time
where the time goes in v10:
time: 25.5 us; the launch traced here: 25.4 us
  Pallas kernels  24.8 us (97%)
  between operations  0.64 us (3%)
    pallas_call x1, Pallas kernels, body(): pl.pallas_call(functools.partial(kernel, n_grp, n_dev, levels, padded, sh...  23.9 us
    pallas_call x1, Pallas kernels, body(): pl.pallas_call(finish, out_shape=(jax.ShapeDtypeStruct((bins, width), F32...  0.84 us

profile of v10, /device:TPU:8, one launch (start us, length us, event | category | flops | bytes accessed | tf_op | source)
XLA Modules:
  0.0 25.4 jit_solution(5035114010396288377)
XLA Ops:
  0.6 23.9 %wave_step.1 = (f32[1152,128]{1,0:T(8,128)S(1)}, f32[3,8,128]{2,1,0:T(8,128)S(1)}, s32[2,512]{1,0:T(2,128)S(1)}) custom-call(f32[1152,128]{1,0:T(8,128)} %bitcast.7, s32[1,128]{1,0:T(1,128)} %mask_hbm.1, f32[2,128]{1,0:T(2,128)} %bitcast.9, f32[2,512]{1,0:T(2,128)} %bitcast.8, s32[1,512]{1,0:T(1,128)} %coup_hbm.1, f32[224,128]{1,0:T(8,128)} %constant.2.clone.tab_hbm), custom_call_target="tpu_custom_call" | custom-call | tf_op jit(solution)/shard_map/wave_step/pallas_call | solution.py:582
  24.6 0.8 %finish.1 = (f32[1152,128]{1,0:T(8,128)}, f32[2,512]{1,0:T(2,128)}) custom-call(f32[1152,128]{1,0:T(8,128)S(1)} %get-tuple-element.7.upd_ref, f32[3,8,128]{2,1,0:T(8,128)S(1)} %get-tuple-element.8.drift, s32[2,512]{1,0:T(2,128)S(1)} %get-tuple-element.9.where_ref), custom_call_target="tpu_custom_call" | custom-call | tf_op jit(solution)/shard_map/finish/pallas_call | solution.py:641

commit v11 on v10

--- a/solution.py
+++ b/solution.py
@@ -315,6 +315,18 @@
         return both
 
     send_far(0)
+    send_far(1)
+    send_far(2)
+
+    link_copies[1].wait_recv()
+    part[0, g, 0:4, :] = cell_sums[4:8] + link[0, 0:4, :]
+    part[0, g, 4:8, :] = link[1, 0:4, :]
+
+    @pl.when(g > 0)
+    def _():
+        for k in range(1, n_grp):
+            group_copy(0, k).start()
+
     near_copy = pltpu.make_async_remote_copy(
         src_ref=ctr,
         dst_ref=near,
@@ -324,17 +336,6 @@
         device_id_type=MESH,
     )
     near_copy.start()
-    send_far(1)
-    send_far(2)
-
-    link_copies[1].wait_recv()
-    part[0, g, 0:4, :] = cell_sums[4:8] + link[0, 0:4, :]
-    part[0, g, 4:8, :] = link[1, 0:4, :]
-
-    @pl.when(g > 0)
-    def _():
-        for k in range(1, n_grp):
-            group_copy(0, k).start()
 
     link_copies[0].wait_recv()
     part[1, g, 0:4, :] = link[2, 0:4, :]

time: 25.5 us -> 25.5 us (level)
  no operation moved by 1% of the time
where the time goes in v11:
time: 25.5 us; the launch traced here: 25.4 us
  Pallas kernels  24.8 us (97%)
  between operations  0.64 us (3%)
    pallas_call x1, Pallas kernels, body(): pl.pallas_call(functools.partial(kernel, n_grp, n_dev, levels, padded, sh...  23.9 us
    pallas_call x1, Pallas kernels, body(): pl.pallas_call(finish, out_shape=(jax.ShapeDtypeStruct((bins, width), F32...  0.84 us

profile of v11, /device:TPU:8, one launch (start us, length us, event | category | flops | bytes accessed | tf_op | source)
XLA Modules:
  0.0 25.4 jit_solution(6537238329269056982)
XLA Ops:
  0.6 23.9 %wave_step.1 = (f32[1152,128]{1,0:T(8,128)S(1)}, f32[3,8,128]{2,1,0:T(8,128)S(1)}, s32[2,512]{1,0:T(2,128)S(1)}) custom-call(f32[1152,128]{1,0:T(8,128)} %bitcast.7, s32[1,128]{1,0:T(1,128)} %mask_hbm.1, f32[2,128]{1,0:T(2,128)} %bitcast.9, f32[2,512]{1,0:T(2,128)} %bitcast.8, s32[1,512]{1,0:T(1,128)} %coup_hbm.1, f32[224,128]{1,0:T(8,128)} %constant.2.clone.tab_hbm), custom_call_target="tpu_custom_call" | custom-call | tf_op jit(solution)/shard_map/wave_step/pallas_call | solution.py:583
  24.6 0.8 %finish.1 = (f32[1152,128]{1,0:T(8,128)}, f32[2,512]{1,0:T(2,128)}) custom-call(f32[1152,128]{1,0:T(8,128)S(1)} %get-tuple-element.7.upd_ref, f32[3,8,128]{2,1,0:T(8,128)S(1)} %get-tuple-element.8.drift, s32[2,512]{1,0:T(2,128)S(1)} %get-tuple-element.9.where_ref), custom_call_target="tpu_custom_call" | custom-call | tf_op jit(solution)/shard_map/finish/pallas_call | solution.py:642
